TPU v7x, 32 devices: a whole 2x2x4 slice. The times are simulated.
32 devices in a mesh: gx: 4 (over z), gy: 4 (over x, core), gz: 2 (over y).
Axes of the slice: x: 2, y: 2, z: 4, core: 2. Of those that a mesh axis runs over, the one named last changes fastest.
Arguments:
- charges: bfloat16 [256, 256, 256], P('gx', 'gy', 'gz'), may hold values from -6 to 6
- taps: float32 [4, 4, 17], replicated, may hold values from 0.05 to 0.3
Outputs:
- potential: bfloat16 [256, 256, 256], P('gx', 'gy', 'gz')
All inputs are finite; a program needn't handle non-finite values.
Results may differ from a plain program's by a relative error of at most 0.012.
The roundings to bfloat16 on the way count: a program that leaves them out, or rounds other values in their place, can miss the bound.
Values may be sent and summed in bfloat16 or wider, within the bound.
No kernel may reach another device: no remote copies, remote signals or barrier semaphores. Data moves between devices by JAX's collectives and lax.ppermute only.
A program may use at most 128 MiB of HBM per device.

v0:
```python
import jax
import jax.numpy as jnp
from jax import lax
from jax.sharding import PartitionSpec as P


def padded_2(value, sides, width):
    for axis, dim in sides:
        count, length = (lax.axis_size(axis), value.shape[dim])
        up = [(i, (i + 1) % count) for i in range(count)]
        down = [(j, i) for i, j in up]
        last = lax.slice_in_dim(value, length - width, length, axis=dim)
        first = lax.slice_in_dim(value, 0, width, axis=dim)
        before = lax.ppermute(last, axis, up)
        after = lax.ppermute(first, axis, down)
        value = jnp.concatenate([before, value, after], axis=dim)
    return value


def restrict_padded(padded):
    for along in range(3):
        fine_count = padded.shape[along] - 6

        def strided(offset):
            return lax.slice_in_dim(padded, 3 + offset, 3 + offset + fine_count, 2, along)

        padded = (
            16.0 * strided(0) + 9.0 * (strided(-1) + strided(1)) - (strided(-3) + strided(3))
        ) / 16.0
    return padded


def prolong_padded(padded):
    for along in range(3):
        coarse_count = padded.shape[along] - 4

        def shifted(start):
            return lax.slice_in_dim(padded, start, start + coarse_count, 1, along)

        centre = shifted(2)
        between = (9.0 * (centre + shifted(3)) - (shifted(1) + shifted(4))) / 16.0
        shape_list = list(centre.shape)
        shape_list[along] = 2 * coarse_count
        padded = jnp.stack([centre, between], along + 1).reshape(shape_list)
    return padded


def widen(field, width):
    return padded_2(field, (("gx", 0), ("gy", 1), ("gz", 2)), width)


def band(tap_row, length):
    row_ids = lax.broadcasted_iota(jnp.int32, (length + 16, length), 0)
    col_ids = lax.broadcasted_iota(jnp.int32, (length + 16, length), 1)
    offsets = row_ids - col_ids
    matrix = jnp.zeros((length + 16, length), jnp.float32)
    for offset in range(tap_row.shape[0]):
        matrix = jnp.where(offsets == offset, tap_row[offset].astype(jnp.float32), matrix)
    return matrix.astype(jnp.bfloat16)


def pick_tile(length):
    if length <= 64:
        return length
    for candidate in (64, 56, 48, 46, 40, 32, 24, 23, 16):
        return candidate
    return length


def pass_along(padded, tap_row, along, length):
    rank_count = padded.ndim
    letters = "abcdefg"[:rank_count]
    tile_len = pick_tile(length)
    if tile_len == length:
        matrix = band(tap_row, length)
        target = letters[:along] + "w" + letters[along + 1 :]
        return jnp.einsum(
            letters + "," + letters[along] + "w->" + target,
            padded,
            matrix,
            preferred_element_type=jnp.float32,
        )
    tile_count = length // tile_len
    matrix = band(tap_row, tile_len)
    widths = [(0, 0)] * rank_count
    widths[along] = (0, tile_len - 16)
    filled = jnp.pad(padded, widths)
    shape_list = list(padded.shape)
    shape_list[along : along + 1] = [tile_count + 1, tile_len]
    tiled = filled.reshape(shape_list)
    leading = lax.slice_in_dim(tiled, 0, tile_count, 1, along)
    trailing = lax.slice_in_dim(
        lax.slice_in_dim(tiled, 1, tile_count + 1, 1, along), 0, 16, 1, along + 1
    )
    source = letters[:along] + "pq" + letters[along + 1 :]
    target = letters[:along] + "pr" + letters[along + 1 :]
    result = jnp.einsum(
        source + ",qr->" + target, leading, matrix[:tile_len], preferred_element_type=jnp.float32
    )
    result = result + jnp.einsum(
        source + ",qr->" + target, trailing, matrix[tile_len:], preferred_element_type=jnp.float32
    )
    out_shape = list(padded.shape)
    out_shape[along] = length
    return result.reshape(out_shape)


def convolve(padded, level_taps, out_x, out_y, out_z):
    potential = jnp.zeros((out_x, out_y, out_z), jnp.float32)
    for term in range(level_taps.shape[0]):
        section = pass_along(padded, level_taps[term], 2, out_z).astype(jnp.bfloat16)
        section = pass_along(section, level_taps[term], 1, out_y).astype(jnp.bfloat16)
        potential = potential + pass_along(section, level_taps[term], 0, out_x)
    return potential


def kernel_local(field, level_taps):
    charged = field.astype(jnp.bfloat16)
    padded = padded_2(charged, (("gx", 0), ("gy", 1), ("gz", 2)), 8)
    potential = convolve(padded, level_taps, field.shape[0], field.shape[1], field.shape[2])
    return potential


def per_device(charges, taps):
    level_taps = taps.astype(jnp.bfloat16)
    level_zero = charges.astype(jnp.float32)
    level_one = restrict_padded(widen(level_zero, 3))
    level_two = restrict_padded(widen(level_one, 3))
    level_three = restrict_padded(widen(level_two, 3))
    kernel_zero = kernel_local(level_zero, level_taps[0])
    kernel_one = kernel_local(level_one, level_taps[1])
    kernel_two = kernel_local(level_two, level_taps[2])
    block_x, block_y, block_z = level_three.shape
    count_x = lax.axis_size("gx")
    count_y = lax.axis_size("gy")
    count_z = lax.axis_size("gz")
    pieces = lax.all_gather(
        level_three.astype(jnp.bfloat16).reshape(1, block_x * block_y * block_z),
        ("gx", "gy", "gz"),
        axis=0,
        tiled=True,
    )
    top_grid = pieces.reshape(count_x, count_y, count_z, block_x, block_y, block_z).transpose(
        0, 3, 1, 4, 2, 5
    )
    top_grid = top_grid.reshape(count_x * block_x, count_y * block_y, count_z * block_z)
    corner = (
        lax.axis_index("gx") * block_x,
        lax.axis_index("gy") * block_y,
        lax.axis_index("gz") * block_z,
    )
    charge_window = lax.dynamic_slice(
        jnp.pad(top_grid, 10, mode="wrap"), corner, (block_x + 20, block_y + 20, block_z + 20)
    )
    window = convolve(charge_window, level_taps[3], block_x + 4, block_y + 4, block_z + 4)
    potential_two = kernel_two + prolong_padded(window)
    potential_one = kernel_one + prolong_padded(widen(potential_two, 2))
    potential_zero = kernel_zero + prolong_padded(widen(potential_one, 2))
    return potential_zero.astype(jnp.bfloat16)


def solution(mesh):
    return jax.shard_map(
        per_device,
        mesh=mesh,
        in_specs=(P("gx", "gy", "gz"), P()),
        out_specs=P("gx", "gy", "gz"),
        check_vma=False,
    )
```

profile of v0, /device:TPU:0, one launch (start us, length us, event | category | flops | bytes accessed | tf_op | source)
XLA Modules:
  0.0 814.1 jit_solution(8965799550738029879)
XLA Ops:
  20.4 10.5 %select_convert_fusion.4 = bf16[80,64]{0,1:T(8,128)(2,1)S(1)} fusion(bf16[]{:T(256)} %bitcast.635, bf16[]{:T(256)} %bitcast.634, bf16[]{:T(256)} %bitcast.633, bf16[]{:T(256)} %bitcast.632, bf16[]{:T(256)} %bitcast.631, bf16[]{:T(256)} %bitcast.630, bf16[]{:T(256)} %bitcast.629, bf16[]{:T(256)} %bitcast.628, bf16[]{:T(256)} %bitcast.627, bf16[]{:T(256)} %bitcast.626, ...), kind=kLoop, calls=%fused_computation.238 | loop fusion | flops 179200 | bytes 10274 | tf_op jit(solution)/shard_map/convert_element_type | solution.py:59
  31.0 11.3 %select_convert_fusion.5 = bf16[80,64]{0,1:T(8,128)(2,1)} fusion(bf16[]{:T(256)} %bitcast.617, bf16[]{:T(256)} %bitcast.616, bf16[]{:T(256)} %bitcast.615, bf16[]{:T(256)} %bitcast.614, bf16[]{:T(256)} %bitcast.613, bf16[]{:T(256)} %bitcast.612, bf16[]{:T(256)} %bitcast.611, bf16[]{:T(256)} %bitcast.610, bf16[]{:T(256)} %bitcast.609, bf16[]{:T(256)} %bitcast.608, ...), kind=kLoop, calls=%fused_computation.239 | loop fusion | flops 179200 | bytes 10274 | tf_op jit(solution)/shard_map/convert_element_type | solution.py:59
  42.3 11.8 %select_convert_fusion.6 = bf16[80,64]{0,1:T(8,128)(2,1)} fusion(bf16[]{:T(256)} %bitcast.599, bf16[]{:T(256)} %bitcast.598, bf16[]{:T(256)} %bitcast.597, bf16[]{:T(256)} %bitcast.596, bf16[]{:T(256)} %bitcast.595, bf16[]{:T(256)} %bitcast.594, bf16[]{:T(256)} %bitcast.593, bf16[]{:T(256)} %bitcast.592, bf16[]{:T(256)} %bitcast.591, bf16[]{:T(256)} %bitcast.590, ...), kind=kLoop, calls=%fused_computation.240 | loop fusion | flops 179200 | bytes 10274 | tf_op jit(solution)/shard_map/convert_element_type | solution.py:59
  54.1 11.3 %select_convert_fusion.7 = bf16[80,64]{0,1:T(8,128)(2,1)} fusion(bf16[]{:T(256)} %bitcast.581, bf16[]{:T(256)} %bitcast.580, bf16[]{:T(256)} %bitcast.579, bf16[]{:T(256)} %bitcast.578, bf16[]{:T(256)} %bitcast.577, bf16[]{:T(256)} %bitcast.576, bf16[]{:T(256)} %bitcast.575, bf16[]{:T(256)} %bitcast.574, bf16[]{:T(256)} %bitcast.573, bf16[]{:T(256)} %bitcast.572, ...), kind=kLoop, calls=%fused_computation.241 | loop fusion | flops 179200 | bytes 10274 | tf_op jit(solution)/shard_map/convert_element_type | solution.py:59
  101.8 7.2 pad_maximum_fusion
  127.5 10.3 %slice.2561 = f32[32,32,64]{2,1,0:T(8,128)S(1)} slice(f32[32,32,134]{2,1,0:T(8,128)S(1)} %subtract_multiply_fusion.1), slice={[0:32:1], [0:32:1], [6:134:2]} | slice | bytes 524288 | tf_op jit(solution)/shard_map/slice | solution.py:25
  137.8 10.6 %slice.2560 = f32[32,32,64]{2,1,0:T(8,128)} slice(f32[32,32,134]{2,1,0:T(8,128)S(1)} %subtract_multiply_fusion.1), slice={[0:32:1], [0:32:1], [0:128:2]} | slice | bytes 524288 | tf_op jit(solution)/shard_map/slice | solution.py:25
  148.4 10.7 %slice.2559 = f32[32,32,64]{2,1,0:T(8,128)} slice(f32[32,32,134]{2,1,0:T(8,128)S(1)} %subtract_multiply_fusion.1), slice={[0:32:1], [0:32:1], [4:132:2]} | slice | bytes 524288 | tf_op jit(solution)/shard_map/slice | solution.py:25
  159.1 10.7 %slice.2558 = f32[32,32,64]{2,1,0:T(8,128)} slice(f32[32,32,134]{2,1,0:T(8,128)S(1)} %subtract_multiply_fusion.1), slice={[0:32:1], [0:32:1], [2:130:2]} | slice | bytes 524288 | tf_op jit(solution)/shard_map/slice | solution.py:25
  169.8 10.8 %slice.2557 = f32[32,32,64]{2,1,0:T(8,128)} slice(f32[32,32,134]{2,1,0:T(8,128)S(1)} %subtract_multiply_fusion.1), slice={[0:32:1], [0:32:1], [3:131:2]} | slice | bytes 524288 | tf_op jit(solution)/shard_map/slice | solution.py:25
  249.1 68.6 %all-gather = bf16[32,1,1024]{2,1,0:T(2,128)(2,1)S(1)} all-gather(bf16[1,1,1024]{2,1,0:T(2,128)(2,1)S(1)} %reshape.1455), channel_id=1, replica_groups=mesh['gx'=4,'gy'=4,'gz'=2] {'gx','gy','gz'}, dimensions={0}, use_global_device_ids=true | all-gather | bytes 67584 | tf_op jit(solution)/shard_map/all_gather | solution.py:137
  322.4 11.1 %convolution_convert_fusion.13 = bf16[28,28,20]{1,2,0:T(8,128)(2,1)S(1)} fusion(bf16[28,28,36]{2,1,0:T(8,128)(2,1)S(1)} %fusion.79, bf16[]{:T(256)} %bitcast.498, bf16[]{:T(256)} %bitcast.497, bf16[]{:T(256)} %bitcast.496, bf16[]{:T(256)} %bitcast.495, bf16[]{:T(256)} %bitcast.494, bf16[]{:T(256)} %bitcast.493, bf16[]{:T(256)} %bitcast.492, bf16[]{:T(256)} %bitcast.491, ...), kind=kOutput, calls=%fused_computation.72 | convolution fusion | flops 1169840 | bytes 87842 | tf_op jit(solution)/shard_map/abc,cw->abw/dot_general | solution.py:77
  333.5 11.0 %fusion.51 = bf16[28,12,20]{0,1,2:T(8,128)(2,1)S(1)} fusion(bf16[28,28,20]{1,2,0:T(8,128)(2,1)S(1)} %convolution_convert_fusion.13, bf16[]{:T(256)} %bitcast.498, bf16[]{:T(256)} %bitcast.497, bf16[]{:T(256)} %bitcast.496, bf16[]{:T(256)} %bitcast.495, bf16[]{:T(256)} %bitcast.494, bf16[]{:T(256)} %bitcast.493, bf16[]{:T(256)} %bitcast.492, bf16[]{:T(256)} %bitcast.491, ...), kind=kOutput, calls=%fused_computation.96 | convolution fusion | flops 394800 | bytes 44834 | tf_op jit(solution)/shard_map/abc,bw->awc/dot_general | solution.py:77
  344.5 11.0 %convolution_convert_fusion.14 = bf16[28,28,20]{1,2,0:T(8,128)(2,1)S(1)} fusion(bf16[28,28,36]{2,1,0:T(8,128)(2,1)S(1)} %fusion.79, bf16[]{:T(256)} %bitcast.461, bf16[]{:T(256)} %bitcast.460, bf16[]{:T(256)} %bitcast.459, bf16[]{:T(256)} %bitcast.458, bf16[]{:T(256)} %bitcast.457, bf16[]{:T(256)} %bitcast.456, bf16[]{:T(256)} %bitcast.455, bf16[]{:T(256)} %bitcast.454, ...), kind=kOutput, calls=%fused_computation.73 | convolution fusion | flops 1169840 | bytes 87842 | tf_op jit(solution)/shard_map/abc,cw->abw/dot_general | solution.py:77
  355.5 10.9 %fusion.50 = bf16[28,12,20]{0,1,2:T(8,128)(2,1)S(1)} fusion(bf16[28,28,20]{1,2,0:T(8,128)(2,1)S(1)} %convolution_convert_fusion.14, bf16[]{:T(256)} %bitcast.461, bf16[]{:T(256)} %bitcast.460, bf16[]{:T(256)} %bitcast.459, bf16[]{:T(256)} %bitcast.458, bf16[]{:T(256)} %bitcast.457, bf16[]{:T(256)} %bitcast.456, bf16[]{:T(256)} %bitcast.455, bf16[]{:T(256)} %bitcast.454, ...), kind=kOutput, calls=%fused_computation.95 | convolution fusion | flops 394800 | bytes 44834 | tf_op jit(solution)/shard_map/abc,bw->awc/dot_general | solution.py:77
  366.5 10.8 %convolution_convert_fusion.15 = bf16[28,28,20]{1,2,0:T(8,128)(2,1)S(1)} fusion(bf16[28,28,36]{2,1,0:T(8,128)(2,1)S(1)} %fusion.79, bf16[]{:T(256)} %bitcast.424, bf16[]{:T(256)} %bitcast.423, bf16[]{:T(256)} %bitcast.422, bf16[]{:T(256)} %bitcast.421, bf16[]{:T(256)} %bitcast.420, bf16[]{:T(256)} %bitcast.419, bf16[]{:T(256)} %bitcast.418, bf16[]{:T(256)} %bitcast.417, ...), kind=kOutput, calls=%fused_computation.74 | convolution fusion | flops 1169840 | bytes 87842 | tf_op jit(solution)/shard_map/abc,cw->abw/dot_general | solution.py:77
  377.2 10.7 %fusion.49 = bf16[28,12,20]{0,1,2:T(8,128)(2,1)S(1)} fusion(bf16[28,28,20]{1,2,0:T(8,128)(2,1)S(1)} %convolution_convert_fusion.15, bf16[]{:T(256)} %bitcast.424, bf16[]{:T(256)} %bitcast.423, bf16[]{:T(256)} %bitcast.422, bf16[]{:T(256)} %bitcast.421, bf16[]{:T(256)} %bitcast.420, bf16[]{:T(256)} %bitcast.419, bf16[]{:T(256)} %bitcast.418, bf16[]{:T(256)} %bitcast.417, ...), kind=kOutput, calls=%fused_computation.94 | convolution fusion | flops 394800 | bytes 44834 | tf_op jit(solution)/shard_map/abc,bw->awc/dot_general | solution.py:77
  387.9 10.6 %convolution_convert_fusion.12 = bf16[28,28,20]{1,2,0:T(8,128)(2,1)S(1)} fusion(bf16[28,28,36]{2,1,0:T(8,128)(2,1)S(1)} %fusion.79, bf16[]{:T(256)} %bitcast.535, bf16[]{:T(256)} %bitcast.534, bf16[]{:T(256)} %bitcast.533, bf16[]{:T(256)} %bitcast.532, bf16[]{:T(256)} %bitcast.531, bf16[]{:T(256)} %bitcast.530, bf16[]{:T(256)} %bitcast.529, bf16[]{:T(256)} %bitcast.528, ...), kind=kOutput, calls=%fused_computation.71 | convolution fusion | flops 1169840 | bytes 87842 | tf_op jit(solution)/shard_map/abc,cw->abw/dot_general | solution.py:77
  398.5 10.5 %fusion.52 = bf16[28,12,20]{0,1,2:T(8,128)(2,1)S(1)} fusion(bf16[28,28,20]{1,2,0:T(8,128)(2,1)S(1)} %convolution_convert_fusion.12, bf16[]{:T(256)} %bitcast.535, bf16[]{:T(256)} %bitcast.534, bf16[]{:T(256)} %bitcast.533, bf16[]{:T(256)} %bitcast.532, bf16[]{:T(256)} %bitcast.531, bf16[]{:T(256)} %bitcast.530, bf16[]{:T(256)} %bitcast.529, bf16[]{:T(256)} %bitcast.528, ...), kind=kOutput, calls=%fused_computation.97 | convolution fusion | flops 394800 | bytes 44834 | tf_op jit(solution)/shard_map/abc,bw->awc/dot_general | solution.py:77
  409.1 10.6 %fusion.104 = f32[12,12,20]{2,0,1:T(8,128)S(1)} fusion(bf16[28,12,20]{0,1,2:T(8,128)(2,1)S(1)} %fusion.49, bf16[]{:T(256)} %bitcast.424, bf16[]{:T(256)} %bitcast.423, bf16[]{:T(256)} %bitcast.422, bf16[]{:T(256)} %bitcast.421, bf16[]{:T(256)} %bitcast.420, bf16[]{:T(256)} %bitcast.419, bf16[]{:T(256)} %bitcast.418, bf16[]{:T(256)} %bitcast.417, ...), kind=kOutput, calls=%fused_computation.210 | convolution fusion | flops 173040 | bytes 24994 | tf_op jit(solution)/shard_map/abc,aw->wbc/dot_general | solution.py:77
  419.7 10.8 %convolution_add_fusion.8 = f32[12,12,20]{2,0,1:T(8,128)S(1)} fusion(f32[12,12,20]{2,0,1:T(8,128)S(1)} %fusion.104, bf16[28,12,20]{0,1,2:T(8,128)(2,1)S(1)} %fusion.50, bf16[]{:T(256)} %bitcast.461, bf16[]{:T(256)} %bitcast.460, bf16[]{:T(256)} %bitcast.459, bf16[]{:T(256)} %bitcast.458, bf16[]{:T(256)} %bitcast.457, bf16[]{:T(256)} %bitcast.456, ...), kind=kOutput, calls=%fused_computation.93 | convolution fusion | flops 175920 | bytes 36514 | tf_op jit(solution)/shard_map/abc,aw->wbc/dot_general | solution.py:77
  430.5 10.9 %convolution_add_fusion.7 = f32[12,12,20]{2,0,1:T(8,128)S(1)} fusion(f32[12,12,20]{2,0,1:T(8,128)S(1)} %convolution_add_fusion.8, bf16[28,12,20]{0,1,2:T(8,128)(2,1)S(1)} %fusion.51, bf16[]{:T(256)} %bitcast.498, bf16[]{:T(256)} %bitcast.497, bf16[]{:T(256)} %bitcast.496, bf16[]{:T(256)} %bitcast.495, bf16[]{:T(256)} %bitcast.494, bf16[]{:T(256)} %bitcast.493, ...), kind=kOutput, calls=%fused_computation.92 | convolution fusion | flops 175920 | bytes 36514 | tf_op jit(solution)/shard_map/abc,aw->wbc/dot_general | solution.py:77
  441.5 10.5 %convolution_add_fusion.6 = f32[12,12,20]{2,0,1:T(8,128)S(1)} fusion(f32[12,12,20]{2,0,1:T(8,128)S(1)} %convolution_add_fusion.7, bf16[28,12,20]{0,1,2:T(8,128)(2,1)S(1)} %fusion.52, bf16[]{:T(256)} %bitcast.535, bf16[]{:T(256)} %bitcast.534, bf16[]{:T(256)} %bitcast.533, bf16[]{:T(256)} %bitcast.532, bf16[]{:T(256)} %bitcast.531, bf16[]{:T(256)} %bitcast.530, ...), kind=kOutput, calls=%fused_computation.91 | convolution fusion | flops 175920 | bytes 36514 | tf_op jit(solution)/shard_map/abc,aw->wbc/dot_general | solution.py:77
  474.6 12.8 %fusion.14 = bf16[80,64,128]{2,1,0:T(8,128)(2,1)} fusion(bf16[80,80,128]{1,2,0:T(8,128)(2,1)S(1)} %bitcast.801, bf16[]{:T(256)} %bitcast.617, bf16[]{:T(256)} %bitcast.616, bf16[]{:T(256)} %bitcast.615, bf16[]{:T(256)} %bitcast.614, bf16[]{:T(256)} %bitcast.613, bf16[]{:T(256)} %bitcast.612, bf16[]{:T(256)} %bitcast.611, bf16[]{:T(256)} %bitcast.610, ...), kind=kOutput, calls=%fused_computation.33 | convolution fusion | flops 105692160 | bytes 2949154 | tf_op jit(solution)/shard_map/abc,bw->awc/dot_general | solution.py:77
  489.2 13.3 %fusion.13 = bf16[80,64,128]{2,1,0:T(8,128)(2,1)} fusion(bf16[80,80,128]{1,2,0:T(8,128)(2,1)S(1)} %bitcast.802, bf16[]{:T(256)} %bitcast.599, bf16[]{:T(256)} %bitcast.598, bf16[]{:T(256)} %bitcast.597, bf16[]{:T(256)} %bitcast.596, bf16[]{:T(256)} %bitcast.595, bf16[]{:T(256)} %bitcast.594, bf16[]{:T(256)} %bitcast.593, bf16[]{:T(256)} %bitcast.592, ...), kind=kOutput, calls=%fused_computation.32 | convolution fusion | flops 105692160 | bytes 2949154 | tf_op jit(solution)/shard_map/abc,bw->awc/dot_general | solution.py:77
  505.9 12.8 %fusion.12 = bf16[80,64,128]{2,1,0:T(8,128)(2,1)} fusion(bf16[80,80,128]{1,2,0:T(8,128)(2,1)S(1)} %bitcast.800, bf16[]{:T(256)} %bitcast.581, bf16[]{:T(256)} %bitcast.580, bf16[]{:T(256)} %bitcast.579, bf16[]{:T(256)} %bitcast.578, bf16[]{:T(256)} %bitcast.577, bf16[]{:T(256)} %bitcast.576, bf16[]{:T(256)} %bitcast.575, bf16[]{:T(256)} %bitcast.574, ...), kind=kOutput, calls=%fused_computation.31 | convolution fusion | flops 105692160 | bytes 2949154 | tf_op jit(solution)/shard_map/abc,bw->awc/dot_general | solution.py:77
  520.1 10.7 %fusion.44 = bf16[32,16,32]{2,1,0:T(8,128)(2,1)S(1)} fusion(bf16[32,32,48]{2,1,0:T(8,128)(2,1)S(1)} %pad_maximum_fusion.21, bf16[]{:T(256)} %bitcast.275, bf16[]{:T(256)} %bitcast.274, bf16[]{:T(256)} %bitcast.273, bf16[]{:T(256)} %bitcast.272, bf16[]{:T(256)} %bitcast.271, bf16[]{:T(256)} %bitcast.270, bf16[]{:T(256)} %bitcast.269, bf16[]{:T(256)} %bitcast.268, ...), kind=kOutput, calls=%fused_computation.79 | convolution fusion | flops 4315136 | bytes 131106 | tf_op jit(solution)/shard_map/abc,bw->awc/dot_general | solution.py:77
  530.8 10.5 %fusion.99 = f32[16,16,32]{2,0,1:T(8,128)S(1)} fusion(bf16[32,16,32]{2,1,0:T(8,128)(2,1)S(1)} %fusion.44, bf16[]{:T(256)} %bitcast.275, bf16[]{:T(256)} %bitcast.274, bf16[]{:T(256)} %bitcast.273, bf16[]{:T(256)} %bitcast.272, bf16[]{:T(256)} %bitcast.271, bf16[]{:T(256)} %bitcast.270, bf16[]{:T(256)} %bitcast.269, bf16[]{:T(256)} %bitcast.268, ...), kind=kOutput, calls=%fused_computation.194 | convolution fusion | flops 542208 | bytes 65570 | tf_op jit(solution)/shard_map/abc,aw->wbc/dot_general | solution.py:77
  541.2 11.6 %fusion.45 = bf16[32,16,32]{2,1,0:T(8,128)(2,1)} fusion(bf16[32,32,48]{2,1,0:T(8,128)(2,1)S(1)} %pad_maximum_fusion.21, bf16[]{:T(256)} %bitcast.312, bf16[]{:T(256)} %bitcast.311, bf16[]{:T(256)} %bitcast.310, bf16[]{:T(256)} %bitcast.309, bf16[]{:T(256)} %bitcast.308, bf16[]{:T(256)} %bitcast.307, bf16[]{:T(256)} %bitcast.306, bf16[]{:T(256)} %bitcast.305, ...), kind=kOutput, calls=%fused_computation.80 | convolution fusion | flops 4315136 | bytes 131106 | tf_op jit(solution)/shard_map/abc,bw->awc/dot_general | solution.py:77
  552.9 11.6 %convolution_add_fusion.5 = f32[16,16,32]{2,0,1:T(8,128)S(1)} fusion(f32[16,16,32]{2,0,1:T(8,128)S(1)} %fusion.99, bf16[32,16,32]{2,1,0:T(8,128)(2,1)} %fusion.45, bf16[]{:T(256)} %bitcast.312, bf16[]{:T(256)} %bitcast.311, bf16[]{:T(256)} %bitcast.310, bf16[]{:T(256)} %bitcast.309, bf16[]{:T(256)} %bitcast.308, bf16[]{:T(256)} %bitcast.307, ...), kind=kOutput, calls=%fused_computation.85 | convolution fusion | flops 550400 | bytes 98338 | tf_op jit(solution)/shard_map/abc,aw->wbc/dot_general | solution.py:77
  564.5 11.6 %fusion.46 = bf16[32,16,32]{2,1,0:T(8,128)(2,1)} fusion(bf16[32,32,48]{2,1,0:T(8,128)(2,1)S(1)} %pad_maximum_fusion.21, bf16[]{:T(256)} %bitcast.349, bf16[]{:T(256)} %bitcast.348, bf16[]{:T(256)} %bitcast.347, bf16[]{:T(256)} %bitcast.346, bf16[]{:T(256)} %bitcast.345, bf16[]{:T(256)} %bitcast.344, bf16[]{:T(256)} %bitcast.343, bf16[]{:T(256)} %bitcast.342, ...), kind=kOutput, calls=%fused_computation.81 | convolution fusion | flops 4315136 | bytes 131106 | tf_op jit(solution)/shard_map/abc,bw->awc/dot_general | solution.py:77
  576.0 11.6 %convolution_add_fusion.4 = f32[16,16,32]{2,0,1:T(8,128)S(1)} fusion(f32[16,16,32]{2,0,1:T(8,128)S(1)} %convolution_add_fusion.5, bf16[32,16,32]{2,1,0:T(8,128)(2,1)} %fusion.46, bf16[]{:T(256)} %bitcast.349, bf16[]{:T(256)} %bitcast.348, bf16[]{:T(256)} %bitcast.347, bf16[]{:T(256)} %bitcast.346, bf16[]{:T(256)} %bitcast.345, bf16[]{:T(256)} %bitcast.344, ...), kind=kOutput, calls=%fused_computation.84 | convolution fusion | flops 550400 | bytes 98338 | tf_op jit(solution)/shard_map/abc,aw->wbc/dot_general | solution.py:77
  587.6 11.7 %fusion.47 = bf16[32,16,32]{2,1,0:T(8,128)(2,1)} fusion(bf16[32,32,48]{2,1,0:T(8,128)(2,1)S(1)} %pad_maximum_fusion.21, bf16[]{:T(256)} %bitcast.386, bf16[]{:T(256)} %bitcast.385, bf16[]{:T(256)} %bitcast.384, bf16[]{:T(256)} %bitcast.383, bf16[]{:T(256)} %bitcast.382, bf16[]{:T(256)} %bitcast.381, bf16[]{:T(256)} %bitcast.380, bf16[]{:T(256)} %bitcast.379, ...), kind=kOutput, calls=%fused_computation.82 | convolution fusion | flops 4315136 | bytes 131106 | tf_op jit(solution)/shard_map/abc,bw->awc/dot_general | solution.py:77
  599.3 11.7 %fusion.48 = f32[16,16,32]{2,0,1:T(8,128)S(1)} fusion(f32[16,16,32]{2,0,1:T(8,128)S(1)} %copy-done.17, f32[16,16,32]{2,0,1:T(8,128)S(1)} %convolution_add_fusion.4, bf16[32,16,32]{2,1,0:T(8,128)(2,1)} %fusion.47, bf16[]{:T(256)} %bitcast.386, bf16[]{:T(256)} %bitcast.385, bf16[]{:T(256)} %bitcast.384, bf16[]{:T(256)} %bitcast.383, bf16[]{:T(256)} %bitcast.382, ...), kind=kOutput, calls=%fused_computation.86 | convolution fusion | flops 558592 | bytes 131106 | tf_op jit(solution)/shard_map/abc,aw->wbc/dot_general | solution.py:77
  615.0 12.6 %fusion.15 = bf16[80,64,128]{2,1,0:T(8,128)(2,1)} fusion(bf16[80,80,128]{1,2,0:T(8,128)(2,1)S(1)} %bitcast.799, bf16[]{:T(256)} %bitcast.635, bf16[]{:T(256)} %bitcast.634, bf16[]{:T(256)} %bitcast.633, bf16[]{:T(256)} %bitcast.632, bf16[]{:T(256)} %bitcast.631, bf16[]{:T(256)} %bitcast.630, bf16[]{:T(256)} %bitcast.629, bf16[]{:T(256)} %bitcast.628, ...), kind=kOutput, calls=%fused_computation.34 | convolution fusion | flops 105692160 | bytes 2949154 | tf_op jit(solution)/shard_map/abc,bw->awc/dot_general | solution.py:77
  632.5 11.2 %fusion.35 = bf16[48,32,64]{2,1,0:T(8,128)(2,1)S(1)} fusion(bf16[48,48,80]{2,1,0:T(8,128)(2,1)S(1)} %pad_maximum_fusion.14, bf16[]{:T(256)} %bitcast.127, bf16[]{:T(256)} %bitcast.126, bf16[]{:T(256)} %bitcast.125, bf16[]{:T(256)} %bitcast.124, bf16[]{:T(256)} %bitcast.123, bf16[]{:T(256)} %bitcast.122, bf16[]{:T(256)} %bitcast.121, bf16[]{:T(256)} %bitcast.120, ...), kind=kOutput, calls=%fused_computation.61 | convolution fusion | flops 33508864 | bytes 565282 | tf_op jit(solution)/shard_map/abc,bw->awc/dot_general | solution.py:77
  643.7 10.8 %fusion.72 = f32[32,32,64]{2,0,1:T(8,128)S(1)} fusion(bf16[48,32,64]{2,1,0:T(8,128)(2,1)S(1)} %fusion.35, bf16[]{:T(256)} %bitcast.127, bf16[]{:T(256)} %bitcast.126, bf16[]{:T(256)} %bitcast.125, bf16[]{:T(256)} %bitcast.124, bf16[]{:T(256)} %bitcast.123, bf16[]{:T(256)} %bitcast.122, bf16[]{:T(256)} %bitcast.121, bf16[]{:T(256)} %bitcast.120, ...), kind=kOutput, calls=%fused_computation.145 | convolution fusion | flops 6345216 | bytes 458786 | tf_op jit(solution)/shard_map/abc,aw->wbc/dot_general | solution.py:77
  654.5 11.3 %fusion.34 = bf16[48,32,64]{2,1,0:T(8,128)(2,1)S(1)} fusion(bf16[48,48,80]{2,1,0:T(8,128)(2,1)S(1)} %pad_maximum_fusion.14, bf16[]{:T(256)} %bitcast.164, bf16[]{:T(256)} %bitcast.163, bf16[]{:T(256)} %bitcast.162, bf16[]{:T(256)} %bitcast.161, bf16[]{:T(256)} %bitcast.160, bf16[]{:T(256)} %bitcast.159, bf16[]{:T(256)} %bitcast.158, bf16[]{:T(256)} %bitcast.157, ...), kind=kOutput, calls=%fused_computation.60 | convolution fusion | flops 33508864 | bytes 565282 | tf_op jit(solution)/shard_map/abc,bw->awc/dot_general | solution.py:77
  665.8 11.0 %convolution_add_fusion.2 = f32[32,32,64]{2,0,1:T(8,128)S(1)} fusion(f32[32,32,64]{2,0,1:T(8,128)S(1)} %fusion.72, bf16[48,32,64]{2,1,0:T(8,128)(2,1)S(1)} %fusion.34, bf16[]{:T(256)} %bitcast.164, bf16[]{:T(256)} %bitcast.163, bf16[]{:T(256)} %bitcast.162, bf16[]{:T(256)} %bitcast.161, bf16[]{:T(256)} %bitcast.160, bf16[]{:T(256)} %bitcast.159, ...), kind=kOutput, calls=%fused_computation.57 | convolution fusion | flops 6410752 | bytes 720930 | tf_op jit(solution)/shard_map/abc,aw->wbc/dot_general | solution.py:77
  676.8 11.2 %fusion.33 = bf16[48,32,64]{2,1,0:T(8,128)(2,1)S(1)} fusion(bf16[48,48,80]{2,1,0:T(8,128)(2,1)S(1)} %pad_maximum_fusion.14, bf16[]{:T(256)} %bitcast.201, bf16[]{:T(256)} %bitcast.200, bf16[]{:T(256)} %bitcast.199, bf16[]{:T(256)} %bitcast.198, bf16[]{:T(256)} %bitcast.197, bf16[]{:T(256)} %bitcast.196, bf16[]{:T(256)} %bitcast.195, bf16[]{:T(256)} %bitcast.194, ...), kind=kOutput, calls=%fused_computation.59 | convolution fusion | flops 33508864 | bytes 565282 | tf_op jit(solution)/shard_map/abc,bw->awc/dot_general | solution.py:77
  688.1 11.7 %convolution_add_fusion.1 = f32[32,32,64]{2,0,1:T(8,128)} fusion(f32[32,32,64]{2,0,1:T(8,128)S(1)} %convolution_add_fusion.2, bf16[48,32,64]{2,1,0:T(8,128)(2,1)S(1)} %fusion.33, bf16[]{:T(256)} %bitcast.201, bf16[]{:T(256)} %bitcast.200, bf16[]{:T(256)} %bitcast.199, bf16[]{:T(256)} %bitcast.198, bf16[]{:T(256)} %bitcast.197, bf16[]{:T(256)} %bitcast.196, ...), kind=kOutput, calls=%fused_computation.56 | convolution fusion | flops 6410752 | bytes 720930 | tf_op jit(solution)/shard_map/abc,aw->wbc/dot_general | solution.py:77
  702.0 12.1 %fusion.32 = bf16[48,32,64]{2,1,0:T(8,128)(2,1)} fusion(bf16[48,48,80]{2,1,0:T(8,128)(2,1)S(1)} %pad_maximum_fusion.14, bf16[]{:T(256)} %bitcast.238, bf16[]{:T(256)} %bitcast.237, bf16[]{:T(256)} %bitcast.236, bf16[]{:T(256)} %bitcast.235, bf16[]{:T(256)} %bitcast.234, bf16[]{:T(256)} %bitcast.233, bf16[]{:T(256)} %bitcast.232, bf16[]{:T(256)} %bitcast.231, ...), kind=kOutput, calls=%fused_computation.58 | convolution fusion | flops 33508864 | bytes 565282 | tf_op jit(solution)/shard_map/abc,bw->awc/dot_general | solution.py:77
  717.5 12.2 %fusion.31 = f32[32,32,64]{2,0,1:T(8,128)S(1)} fusion(f32[32,32,64]{2,0,1:T(8,128)S(1)} %copy.206, f32[32,32,64]{2,0,1:T(8,128)} %convolution_add_fusion.1, bf16[48,32,64]{2,1,0:T(8,128)(2,1)} %fusion.32, bf16[]{:T(256)} %bitcast.238, bf16[]{:T(256)} %bitcast.237, bf16[]{:T(256)} %bitcast.236, bf16[]{:T(256)} %bitcast.235, bf16[]{:T(256)} %bitcast.234, ...), kind=kOutput, calls=%fused_computation.55 | convolution fusion | flops 6476288 | bytes 983074 | tf_op jit(solution)/shard_map/abc,aw->wbc/dot_general | solution.py:77
  733.6 13.0 %fusion.17 = f32[64,64,128]{2,0,1:T(8,128)} fusion(bf16[80,64,128]{2,1,0:T(8,128)(2,1)S(1)} %copy-done.6, bf16[]{:T(256)} %bitcast.617, bf16[]{:T(256)} %bitcast.616, bf16[]{:T(256)} %bitcast.615, bf16[]{:T(256)} %bitcast.614, bf16[]{:T(256)} %bitcast.613, bf16[]{:T(256)} %bitcast.612, bf16[]{:T(256)} %bitcast.611, bf16[]{:T(256)} %bitcast.610, ...), kind=kOutput, calls=%fused_computation.40 | convolution fusion | flops 84065280 | bytes 3407906 | tf_op jit(solution)/shard_map/abc,aw->wbc/dot_general | solution.py:77
  748.7 13.6 %fusion.19 = f32[64,64,128]{2,0,1:T(8,128)} fusion(bf16[80,64,128]{2,1,0:T(8,128)(2,1)S(1)} %copy-done.5, bf16[]{:T(256)} %bitcast.599, bf16[]{:T(256)} %bitcast.598, bf16[]{:T(256)} %bitcast.597, bf16[]{:T(256)} %bitcast.596, bf16[]{:T(256)} %bitcast.595, bf16[]{:T(256)} %bitcast.594, bf16[]{:T(256)} %bitcast.593, bf16[]{:T(256)} %bitcast.592, ...), kind=kOutput, calls=%fused_computation.42 | convolution fusion | flops 84065280 | bytes 3407906 | tf_op jit(solution)/shard_map/abc,aw->wbc/dot_general | solution.py:77
  765.4 13.0 %fusion.21 = f32[64,64,128]{2,0,1:T(8,128)} fusion(bf16[80,64,128]{2,1,0:T(8,128)(2,1)S(1)} %copy-done.4, bf16[]{:T(256)} %bitcast.581, bf16[]{:T(256)} %bitcast.580, bf16[]{:T(256)} %bitcast.579, bf16[]{:T(256)} %bitcast.578, bf16[]{:T(256)} %bitcast.577, bf16[]{:T(256)} %bitcast.576, bf16[]{:T(256)} %bitcast.575, bf16[]{:T(256)} %bitcast.574, ...), kind=kOutput, calls=%fused_computation.44 | convolution fusion | flops 84065280 | bytes 3407906 | tf_op jit(solution)/shard_map/abc,aw->wbc/dot_general | solution.py:77
  786.5 6.2 copy.215
  797.3 14.8 %add_convert_fusion.4 = bf16[64,64,128]{2,0,1:T(8,128)(2,1)S(1)} fusion(f32[64,64,128]{2,0,1:T(8,128)S(1)} %copy.216, f32[64,64,128]{2,0,1:T(8,128)} %fusion.17, f32[64,64,128]{2,0,1:T(8,128)} %fusion.21, f32[64,64,128]{2,0,1:T(8,128)} %fusion.19, bf16[80,64,128]{2,1,0:T(8,128)(2,1)S(1)} %copy-done.3, bf16[]{:T(256)} %bitcast.635, bf16[]{:T(256)} %bitcast.634, ...), kind=kOutput, calls=%fused_computation.16 | convolution fusion | flops 86686720 | bytes 10747938 | tf_op jit(solution)/shard_map/abc,aw->wbc/dot_general | solution.py:77
  (318 shorter events, 214.8 us)
Async XLA Ops:
  1.5 67.4 %collective-permute-start.6 = (f32[3,64,128]{2,1,0:T(8,128)}, f32[3,64,128]{2,1,0:T(8,128)S(1)}, u32[]{:S(2)}, u32[]{:S(2)}) collective-permute-start(f32[3,64,128]{2,1,0:T(8,128)} %get-tuple-element.25), channel_id=1, source_target_pairs={{0,8},{8,16},{16,24},{24,0},{1,9},{9,17},{17,25},{25,1},{2,10},{10... | collective-permute-start | bytes 294920 | tf_op jit(solution)/shard_map/ppermute | solution.py:14
  4.6 64.3 %collective-permute-start.7 = (f32[3,64,128]{2,1,0:T(8,128)}, f32[3,64,128]{2,1,0:T(8,128)}, u32[]{:S(2)}, u32[]{:S(2)}) collective-permute-start(f32[3,64,128]{2,1,0:T(8,128)} %get-tuple-element.26), channel_id=1, source_target_pairs={{8,0},{16,8},{24,16},{0,24},{9,1},{17,9},{25,17},{1,25},{10,2},{18... | collective-permute-start | bytes 294920 | tf_op jit(solution)/shard_map/ppermute | solution.py:15
  8.2 63.2 %collective-permute-start.1 = (bf16[8,64,128]{2,1,0:T(8,128)(2,1)}, bf16[8,64,128]{2,1,0:T(8,128)(2,1)}, u32[]{:S(2)}, u32[]{:S(2)}) collective-permute-start(bf16[8,64,128]{2,1,0:T(8,128)(2,1)} %get-tuple-element.21), channel_id=1, source_target_pairs={{8,0},{16,8},{24,16},{0,24},{9,1},{17,9},{25,17},{1,25},{10,2},{18... | collective-permute-start | bytes 393224 | tf_op jit(solution)/shard_map/ppermute | solution.py:15
  10.3 56.6 %collective-permute-start = (bf16[8,64,128]{2,1,0:T(8,128)(2,1)S(1)}, bf16[8,64,128]{2,1,0:T(8,128)(2,1)S(1)}, u32[]{:S(2)}, u32[]{:S(2)}) collective-permute-start(bf16[8,64,128]{2,1,0:T(8,128)(2,1)S(1)} %get-tuple-element.22), channel_id=1, source_target_pairs={{0,8},{8,16},{16,24},{24,0},{1,9},{9,17},{17,25},{25,1},{2,10},{10... | collective-permute-start | bytes 393224 | tf_op jit(solution)/shard_map/ppermute | solution.py:14
  69.7 5.4 collective-permute-start.8
  69.7 5.3 collective-permute-start.9
  73.3 16.0 %collective-permute-start.2 = (bf16[80,8,128]{2,1,0:T(8,128)(2,1)}, bf16[80,8,128]{2,1,0:T(8,128)(2,1)}, u32[]{:S(2)}, u32[]{:S(2)}) collective-permute-start(bf16[80,8,128]{2,1,0:T(8,128)(2,1)} %get-tuple-element.17), channel_id=1, source_target_pairs={{0,2},{2,4},{4,6},{6,0},{1,3},{3,5},{5,7},{7,1},{8,10},{10,12},{12... | collective-permute-start | bytes 491528 | tf_op jit(solution)/shard_map/ppermute | solution.py:14
  73.4 15.9 %collective-permute-start.3 = (bf16[80,8,128]{2,1,0:T(8,128)(2,1)}, bf16[80,8,128]{2,1,0:T(8,128)(2,1)}, u32[]{:S(2)}, u32[]{:S(2)}) collective-permute-start(bf16[80,8,128]{2,1,0:T(8,128)(2,1)} %get-tuple-element.18), channel_id=1, source_target_pairs={{2,0},{4,2},{6,4},{0,6},{3,1},{5,3},{7,5},{1,7},{10,8},{12,10},{14... | collective-permute-start | bytes 491528 | tf_op jit(solution)/shard_map/ppermute | solution.py:15
  87.3 11.3 %collective-permute-start.11 = (f32[70,70,3]{1,0,2:T(8,128)}, f32[70,70,3]{1,0,2:T(8,128)}, u32[]{:S(2)}, u32[]{:S(2)}) collective-permute-start(f32[70,70,3]{1,0,2:T(8,128)} %copy.167), channel_id=1, source_target_pairs={{1,0},{0,1},{3,2},{2,3},{5,4},{4,5},{7,6},{6,7},{9,8},{8,9},{11,10... | collective-permute-start | bytes 176408 | tf_op jit(solution)/shard_map/ppermute | solution.py:15
  89.0 6.3 collective-permute-start.10
  182.4 11.9 %collective-permute-start.18 = (f32[3,32,64]{2,1,0:T(8,128)S(1)}, f32[3,32,64]{2,1,0:T(8,128)S(1)}, u32[]{:S(2)}, u32[]{:S(2)}) collective-permute-start(f32[3,32,64]{2,1,0:T(8,128)S(1)} %get-tuple-element.45), channel_id=1, source_target_pairs={{0,8},{8,16},{16,24},{24,0},{1,9},{9,17},{17,25},{25,1},{2,10},{10... | collective-permute-start | bytes 73736 | tf_op jit(solution)/shard_map/ppermute | solution.py:14
  182.5 11.8 %collective-permute-start.19 = (f32[3,32,64]{2,1,0:T(8,128)S(1)}, f32[3,32,64]{2,1,0:T(8,128)S(1)}, u32[]{:S(2)}, u32[]{:S(2)}) collective-permute-start(f32[3,32,64]{2,1,0:T(8,128)S(1)} %get-tuple-element.46), channel_id=1, source_target_pairs={{8,0},{16,8},{24,16},{0,24},{9,1},{17,9},{25,17},{1,25},{10,2},{18... | collective-permute-start | bytes 73736 | tf_op jit(solution)/shard_map/ppermute | solution.py:15
  192.3 267.4 %collective-permute-start.5 = (bf16[80,80,8]{1,2,0:T(8,128)(2,1)}, bf16[80,80,8]{1,2,0:T(8,128)(2,1)}, u32[]{:S(2)}, u32[]{:S(2)}) collective-permute-start(bf16[80,80,8]{1,2,0:T(8,128)(2,1)} %copy.150), channel_id=1, source_target_pairs={{1,0},{0,1},{3,2},{2,3},{5,4},{4,5},{7,6},{6,7},{9,8},{8,9},{11,10... | collective-permute-start | bytes 307208 | tf_op jit(solution)/shard_map/ppermute | solution.py:15
  193.8 263.5 %collective-permute-start.4 = (bf16[80,80,8]{1,2,0:T(8,128)(2,1)}, bf16[80,80,8]{1,2,0:T(8,128)(2,1)}, u32[]{:S(2)}, u32[]{:S(2)}) collective-permute-start(bf16[80,80,8]{1,2,0:T(8,128)(2,1)} %copy.149), channel_id=1, source_target_pairs={{0,1},{1,0},{2,3},{3,2},{4,5},{5,4},{6,7},{7,6},{8,9},{9,8},{10,11... | collective-permute-start | bytes 307208 | tf_op jit(solution)/shard_map/ppermute | solution.py:14
  194.4 3.9 collective-permute-start.20
  194.4 5.6 collective-permute-start.21
  196.2 6.6 collective-permute-start.12
  198.3 5.7 collective-permute-start.13
  201.2 6.2 collective-permute-start.23
  202.8 4.2 collective-permute-start.22
  204.0 24.3 %collective-permute-start.14 = (bf16[48,8,64]{2,1,0:T(8,128)(2,1)S(1)}, bf16[48,8,64]{2,1,0:T(8,128)(2,1)S(1)}, u32[]{:S(2)}, u32[]{:S(2)}) collective-permute-start(bf16[48,8,64]{2,1,0:T(8,128)(2,1)S(1)} %get-tuple-element.49), channel_id=1, source_target_pairs={{0,2},{2,4},{4,6},{6,0},{1,3},{3,5},{5,7},{7,1},{8,10},{10,12},{12... | collective-permute-start | bytes 147464 | tf_op jit(solution)/shard_map/ppermute | solution.py:14
  215.6 5.8 collective-permute-start.30
  215.8 5.5 collective-permute-start.31
  221.3 5.7 collective-permute-start.24
  221.3 5.7 collective-permute-start.25
  227.0 2.6 collective-permute-start.15
  227.1 4.3 collective-permute-start.32
  228.3 3.0 collective-permute-start.33
  229.6 223.8 %collective-permute-start.26 = (bf16[32,8,32]{2,1,0:T(8,128)(2,1)}, bf16[32,8,32]{2,1,0:T(8,128)(2,1)}, u32[]{:S(2)}, u32[]{:S(2)}) collective-permute-start(bf16[32,8,32]{2,1,0:T(8,128)(2,1)} %get-tuple-element.71), channel_id=1, source_target_pairs={{0,2},{2,4},{4,6},{6,0},{1,3},{3,5},{5,7},{7,1},{8,10},{10,12},{12... | collective-permute-start | bytes 49160 | tf_op jit(solution)/shard_map/ppermute | solution.py:14
  231.5 9.2 %collective-permute-start.34 = (f32[22,22,3]{2,1,0:T(8,128)S(1)}, f32[22,22,3]{2,1,0:T(8,128)S(1)}, u32[]{:S(2)}, u32[]{:S(2)}) collective-permute-start(f32[22,22,3]{2,1,0:T(8,128)S(1)} %get-tuple-element.53), channel_id=1, source_target_pairs={{0,1},{1,0},{2,3},{3,2},{4,5},{5,4},{6,7},{7,6},{8,9},{9,8},{10,11... | collective-permute-start | bytes 17432 | tf_op jit(solution)/shard_map/ppermute | solution.py:14
  232.7 13.8 %collective-permute-start.35 = (f32[22,22,3]{2,1,0:T(8,128)S(1)}, f32[22,22,3]{2,1,0:T(8,128)S(1)}, u32[]{:S(2)}, u32[]{:S(2)}) collective-permute-start(f32[22,22,3]{2,1,0:T(8,128)S(1)} %get-tuple-element.54), channel_id=1, source_target_pairs={{1,0},{0,1},{3,2},{2,3},{5,4},{4,5},{7,6},{6,7},{9,8},{8,9},{11,10... | collective-permute-start | bytes 17432 | tf_op jit(solution)/shard_map/ppermute | solution.py:15
  240.7 212.7 %collective-permute-start.27 = (bf16[32,8,32]{2,1,0:T(8,128)(2,1)}, bf16[32,8,32]{2,1,0:T(8,128)(2,1)}, u32[]{:S(2)}, u32[]{:S(2)}) collective-permute-start(bf16[32,8,32]{2,1,0:T(8,128)(2,1)} %get-tuple-element.72), channel_id=1, source_target_pairs={{2,0},{4,2},{6,4},{0,6},{3,1},{5,3},{7,5},{1,7},{10,8},{12,10},{14... | collective-permute-start | bytes 49160 | tf_op jit(solution)/shard_map/ppermute | solution.py:15
  246.5 384.2 %collective-permute-start.17 = (bf16[48,48,8]{1,2,0:T(8,128)(2,1)}, bf16[48,48,8]{1,2,0:T(8,128)(2,1)}, u32[]{:S(2)}, u32[]{:S(2)}) collective-permute-start(bf16[48,48,8]{1,2,0:T(8,128)(2,1)} %copy.171), channel_id=1, source_target_pairs={{1,0},{0,1},{3,2},{2,3},{5,4},{4,5},{7,6},{6,7},{9,8},{8,9},{11,10... | collective-permute-start | bytes 110600 | tf_op jit(solution)/shard_map/ppermute | solution.py:15
  453.4 176.0 %collective-permute-start.16 = (bf16[48,48,8]{1,2,0:T(8,128)(2,1)}, bf16[48,48,8]{1,2,0:T(8,128)(2,1)}, u32[]{:S(2)}, u32[]{:S(2)}) collective-permute-start(bf16[48,48,8]{1,2,0:T(8,128)(2,1)} %copy.170), channel_id=1, source_target_pairs={{0,1},{1,0},{2,3},{3,2},{4,5},{5,4},{6,7},{7,6},{8,9},{9,8},{10,11... | collective-permute-start | bytes 110600 | tf_op jit(solution)/shard_map/ppermute | solution.py:14
  455.3 63.3 %collective-permute-start.28 = (bf16[32,32,8]{2,1,0:T(8,128)(2,1)}, bf16[32,32,8]{2,1,0:T(8,128)(2,1)}, u32[]{:S(2)}, u32[]{:S(2)}) collective-permute-start(bf16[32,32,8]{2,1,0:T(8,128)(2,1)} %get-tuple-element.57), channel_id=1, source_target_pairs={{0,1},{1,0},{2,3},{3,2},{4,5},{5,4},{6,7},{7,6},{8,9},{9,8},{10,11... | collective-permute-start | bytes 49160 | tf_op jit(solution)/shard_map/ppermute | solution.py:14
  457.3 61.3 %collective-permute-start.29 = (bf16[32,32,8]{2,1,0:T(8,128)(2,1)}, bf16[32,32,8]{2,1,0:T(8,128)(2,1)}, u32[]{:S(2)}, u32[]{:S(2)}) collective-permute-start(bf16[32,32,8]{2,1,0:T(8,128)(2,1)} %get-tuple-element.58), channel_id=1, source_target_pairs={{1,0},{0,1},{3,2},{2,3},{5,4},{4,5},{7,6},{6,7},{9,8},{8,9},{11,10... | collective-permute-start | bytes 49160 | tf_op jit(solution)/shard_map/ppermute | solution.py:15
  611.0 16.7 %collective-permute-start.36 = (f32[2,16,32]{2,0,1:T(2,128)S(1)}, f32[2,16,32]{2,0,1:T(2,128)S(1)}, u32[]{:S(2)}, u32[]{:S(2)}) collective-permute-start(f32[2,16,32]{2,0,1:T(2,128)S(1)} %get-tuple-element.69), channel_id=1, source_target_pairs={{0,8},{8,16},{16,24},{24,0},{1,9},{9,17},{17,25},{25,1},{2,10},{10... | collective-permute-start | bytes 12296 | tf_op jit(solution)/shard_map/ppermute | solution.py:14
  611.1 16.6 %collective-permute-start.37 = (f32[2,16,32]{2,0,1:T(2,128)S(1)}, f32[2,16,32]{2,0,1:T(2,128)S(1)}, u32[]{:S(2)}, u32[]{:S(2)}) collective-permute-start(f32[2,16,32]{2,0,1:T(2,128)S(1)} %get-tuple-element.70), channel_id=1, source_target_pairs={{8,0},{16,8},{24,16},{0,24},{9,1},{17,9},{25,17},{1,25},{10,2},{18... | collective-permute-start | bytes 12296 | tf_op jit(solution)/shard_map/ppermute | solution.py:15
  627.7 72.0 %collective-permute-start.38 = (f32[20,2,32]{2,0,1:T(8,128)S(1)}, f32[20,2,32]{2,0,1:T(8,128)S(1)}, u32[]{:S(2)}, u32[]{:S(2)}) collective-permute-start(f32[20,2,32]{2,0,1:T(8,128)S(1)} %get-tuple-element.67), channel_id=1, source_target_pairs={{0,2},{2,4},{4,6},{6,0},{1,3},{3,5},{5,7},{7,1},{8,10},{10,12},{12... | collective-permute-start | bytes 15368 | tf_op jit(solution)/shard_map/ppermute | solution.py:14
  627.8 72.0 %collective-permute-start.39 = (f32[20,2,32]{2,0,1:T(8,128)S(1)}, f32[20,2,32]{2,0,1:T(8,128)S(1)}, u32[]{:S(2)}, u32[]{:S(2)}) collective-permute-start(f32[20,2,32]{2,0,1:T(8,128)S(1)} %get-tuple-element.68), channel_id=1, source_target_pairs={{2,0},{4,2},{6,4},{0,6},{3,1},{5,3},{7,5},{1,7},{10,8},{12,10},{14... | collective-permute-start | bytes 15368 | tf_op jit(solution)/shard_map/ppermute | solution.py:15
  699.9 14.2 %collective-permute-start.40 = (f32[20,20,2]{2,0,1:T(8,128)S(1)}, f32[20,20,2]{2,0,1:T(8,128)S(1)}, u32[]{:S(2)}, u32[]{:S(2)}) collective-permute-start(f32[20,20,2]{2,0,1:T(8,128)S(1)} %get-tuple-element.63), channel_id=1, source_target_pairs={{0,1},{1,0},{2,3},{3,2},{4,5},{5,4},{6,7},{7,6},{8,9},{9,8},{10,11... | collective-permute-start | bytes 9608 | tf_op jit(solution)/shard_map/ppermute | solution.py:14
  702.0 12.2 %collective-permute-start.41 = (f32[20,20,2]{2,0,1:T(8,128)S(1)}, f32[20,20,2]{2,0,1:T(8,128)S(1)}, u32[]{:S(2)}, u32[]{:S(2)}) collective-permute-start(f32[20,20,2]{2,0,1:T(8,128)S(1)} %get-tuple-element.64), channel_id=1, source_target_pairs={{1,0},{0,1},{3,2},{2,3},{5,4},{4,5},{7,6},{6,7},{9,8},{8,9},{11,10... | collective-permute-start | bytes 9608 | tf_op jit(solution)/shard_map/ppermute | solution.py:15
  729.7 16.9 %collective-permute-start.42 = (f32[2,32,64]{2,0,1:T(2,128)S(1)}, f32[2,32,64]{2,0,1:T(2,128)S(1)}, u32[]{:S(2)}, u32[]{:S(2)}) collective-permute-start(f32[2,32,64]{2,0,1:T(2,128)S(1)} %get-tuple-element.41), channel_id=1, source_target_pairs={{0,8},{8,16},{16,24},{24,0},{1,9},{9,17},{17,25},{25,1},{2,10},{10... | collective-permute-start | bytes 49160 | tf_op jit(solution)/shard_map/ppermute | solution.py:14
  729.8 16.9 %collective-permute-start.43 = (f32[2,32,64]{2,0,1:T(2,128)S(1)}, f32[2,32,64]{2,0,1:T(2,128)S(1)}, u32[]{:S(2)}, u32[]{:S(2)}) collective-permute-start(f32[2,32,64]{2,0,1:T(2,128)S(1)} %get-tuple-element.42), channel_id=1, source_target_pairs={{8,0},{16,8},{24,16},{0,24},{9,1},{17,9},{25,17},{1,25},{10,2},{18... | collective-permute-start | bytes 49160 | tf_op jit(solution)/shard_map/ppermute | solution.py:15
  746.7 15.6 %collective-permute-start.44 = (f32[36,2,64]{2,0,1:T(8,128)S(1)}, f32[36,2,64]{2,0,1:T(8,128)S(1)}, u32[]{:S(2)}, u32[]{:S(2)}) collective-permute-start(f32[36,2,64]{2,0,1:T(8,128)S(1)} %get-tuple-element.37), channel_id=1, source_target_pairs={{0,2},{2,4},{4,6},{6,0},{1,3},{3,5},{5,7},{7,1},{8,10},{10,12},{12... | collective-permute-start | bytes 55304 | tf_op jit(solution)/shard_map/ppermute | solution.py:14
  746.7 15.5 %collective-permute-start.45 = (f32[36,2,64]{2,0,1:T(8,128)S(1)}, f32[36,2,64]{2,0,1:T(8,128)S(1)}, u32[]{:S(2)}, u32[]{:S(2)}) collective-permute-start(f32[36,2,64]{2,0,1:T(8,128)S(1)} %get-tuple-element.38), channel_id=1, source_target_pairs={{2,0},{4,2},{6,4},{0,6},{3,1},{5,3},{7,5},{1,7},{10,8},{12,10},{14... | collective-permute-start | bytes 55304 | tf_op jit(solution)/shard_map/ppermute | solution.py:15
  763.3 15.5 %collective-permute-start.47 = (f32[36,36,2]{1,2,0:T(2,128)S(1)}, f32[36,36,2]{1,2,0:T(2,128)S(1)}, u32[]{:S(2)}, u32[]{:S(2)}) collective-permute-start(f32[36,36,2]{1,2,0:T(2,128)S(1)} %copy.208), channel_id=1, source_target_pairs={{1,0},{0,1},{3,2},{2,3},{5,4},{4,5},{7,6},{6,7},{9,8},{8,9},{11,10... | collective-permute-start | bytes 31112 | tf_op jit(solution)/shard_map/ppermute | solution.py:15
  765.3 13.1 %collective-permute-start.46 = (f32[36,36,2]{1,2,0:T(2,128)S(1)}, f32[36,36,2]{1,2,0:T(2,128)S(1)}, u32[]{:S(2)}, u32[]{:S(2)}) collective-permute-start(f32[36,36,2]{1,2,0:T(2,128)S(1)} %copy.207), channel_id=1, source_target_pairs={{0,1},{1,0},{2,3},{3,2},{4,5},{5,4},{6,7},{7,6},{8,9},{9,8},{10,11... | collective-permute-start | bytes 31112 | tf_op jit(solution)/shard_map/ppermute | solution.py:14
  (29 other events, 1071.7 us)
where the time goes:
time: 826 us; the launch traced here: 814 us
  matrix products  425 us (51%)
  local copies, waits for them, and re-layouts  155 us (19%)
  other arithmetic  84 us (10%)
  blocking collectives  68.6 us (8%)
  starting transfers between devices  58.2 us (7%)
  waiting for transfers between devices  22.3 us (3%)
    dot_general x36, matrix products, pass_along(): jnp.einsum(letters + ',' + letters[along] + 'w->' + target, padded, matri...  418 us
    slice x30, local copies, waits for them, and re-layouts, strided(): lax.slice_in_dim(padded, 3 + offset, 3 + offset + fine_count, 2, along)  75.9 us
    all_gather x1, blocking collectives, per_device(): lax.all_gather(level_three.astype(jnp.bfloat16).reshape(1, block_x * bloc...  68.6 us
    ppermute x24, starting transfers between devices, padded_2(): after = lax.ppermute(first, axis, down)  45 us
    convert_element_type x4, other arithmetic, band(): return matrix.astype(jnp.bfloat16)  44.9 us
    concatenate x17, other arithmetic, padded_2(): value = jnp.concatenate([before, value, after], axis=dim)  20.3 us
    slice x22, local copies, waits for them, and re-layouts, padded_2(): last = lax.slice_in_dim(value, length - width, length, axis=dim)  17.6 us
    ppermute x24, waiting for transfers between devices, padded_2(): before = lax.ppermute(last, axis, up)  17.5 us
  transfers between devices with their start and end apart: 48, of which 7 were waited for; matrix products, arithmetic and copies ran while one was open for 65% of the time, Pallas kernels for 0%

commit v1 on v0

--- a/solution.py
+++ b/solution.py
@@ -134,11 +134,17 @@
     count_x = lax.axis_size("gx")
     count_y = lax.axis_size("gy")
     count_z = lax.axis_size("gz")
-    pieces = lax.all_gather(
-        level_three.astype(jnp.bfloat16).reshape(1, block_x * block_y * block_z),
-        ("gx", "gy", "gz"),
+    pieces = jnp.concatenate(
+        lax.all_to_all(
+            jnp.stack(
+                [level_three.astype(jnp.bfloat16).reshape(1, block_x * block_y * block_z)]
+                * lax.axis_size(("gx", "gy", "gz"))
+            ),
+            ("gx", "gy", "gz"),
+            0,
+            0,
+        ),
         axis=0,
-        tiled=True,
     )
     top_grid = pieces.reshape(count_x, count_y, count_z, block_x, block_y, block_z).transpose(
         0, 3, 1, 4, 2, 5

time: 826 us -> 773 us (0.936)
  blocking collectives: 68.6 us -> 0 us
    all_gather x1 -> x0, blocking collectives: 68.6 us -> none  [per_device(): lax.all_gather(level_three.astype(jnp.bfloat16).reshape(1, block_x * bloc...]
  transfers between devices with their start and end apart: 48 -> 49, of which waited for: 7 -> 8; matrix products, arithmetic and copies ran while one was open for 65% -> 50% of each run, Pallas kernels for 0% -> 0%
where the time goes in v1:
time: 773 us; the launch traced here: 761 us
  matrix products  423 us (55%)
  local copies, waits for them, and re-layouts  163 us (21%)
  other arithmetic  84.7 us (11%)
  starting transfers between devices  64 us (8%)
  waiting for transfers between devices  24 us (3%)
    dot_general x36, matrix products, pass_along(): jnp.einsum(letters + ',' + letters[along] + 'w->' + target, padded, matri...  416 us
    slice x30, local copies, waits for them, and re-layouts, strided(): lax.slice_in_dim(padded, 3 + offset, 3 + offset + fine_count, 2, along)  75.8 us
    convert_element_type x4, other arithmetic, band(): return matrix.astype(jnp.bfloat16)  44.6 us
    ppermute x24, starting transfers between devices, padded_2(): after = lax.ppermute(first, axis, down)  44.1 us
    concatenate x17, other arithmetic, padded_2(): value = jnp.concatenate([before, value, after], axis=dim)  20.3 us
    slice x22, local copies, waits for them, and re-layouts, padded_2(): last = lax.slice_in_dim(value, length - width, length, axis=dim)  19 us
    ppermute x24, waiting for transfers between devices, padded_2(): before = lax.ppermute(last, axis, up)  17.9 us
  transfers between devices with their start and end apart: 49, of which 8 were waited for; matrix products, arithmetic and copies ran while one was open for 50% of the time, Pallas kernels for 0%

profile of v1, /device:TPU:0, one launch (start us, length us, event | category | flops | bytes accessed | tf_op | source)
XLA Modules:
  0.0 760.6 jit_solution(2187248637277075908)
XLA Ops:
  20.4 10.8 %select_convert_fusion.4 = bf16[80,64]{0,1:T(8,128)(2,1)S(1)} fusion(bf16[]{:T(256)} %bitcast.635, bf16[]{:T(256)} %bitcast.634, bf16[]{:T(256)} %bitcast.633, bf16[]{:T(256)} %bitcast.632, bf16[]{:T(256)} %bitcast.631, bf16[]{:T(256)} %bitcast.630, bf16[]{:T(256)} %bitcast.629, bf16[]{:T(256)} %bitcast.628, bf16[]{:T(256)} %bitcast.627, bf16[]{:T(256)} %bitcast.626, ...), kind=kLoop, calls=%fused_computation.238 | loop fusion | flops 179200 | bytes 10274 | tf_op jit(solution)/shard_map/convert_element_type | solution.py:59
  31.2 11.4 %select_convert_fusion.5 = bf16[80,64]{0,1:T(8,128)(2,1)} fusion(bf16[]{:T(256)} %bitcast.617, bf16[]{:T(256)} %bitcast.616, bf16[]{:T(256)} %bitcast.615, bf16[]{:T(256)} %bitcast.614, bf16[]{:T(256)} %bitcast.613, bf16[]{:T(256)} %bitcast.612, bf16[]{:T(256)} %bitcast.611, bf16[]{:T(256)} %bitcast.610, bf16[]{:T(256)} %bitcast.609, bf16[]{:T(256)} %bitcast.608, ...), kind=kLoop, calls=%fused_computation.239 | loop fusion | flops 179200 | bytes 10274 | tf_op jit(solution)/shard_map/convert_element_type | solution.py:59
  42.5 11.2 %select_convert_fusion.6 = bf16[80,64]{0,1:T(8,128)(2,1)} fusion(bf16[]{:T(256)} %bitcast.599, bf16[]{:T(256)} %bitcast.598, bf16[]{:T(256)} %bitcast.597, bf16[]{:T(256)} %bitcast.596, bf16[]{:T(256)} %bitcast.595, bf16[]{:T(256)} %bitcast.594, bf16[]{:T(256)} %bitcast.593, bf16[]{:T(256)} %bitcast.592, bf16[]{:T(256)} %bitcast.591, bf16[]{:T(256)} %bitcast.590, ...), kind=kLoop, calls=%fused_computation.240 | loop fusion | flops 179200 | bytes 10274 | tf_op jit(solution)/shard_map/convert_element_type | solution.py:59
  53.7 11.2 %select_convert_fusion.7 = bf16[80,64]{0,1:T(8,128)(2,1)} fusion(bf16[]{:T(256)} %bitcast.581, bf16[]{:T(256)} %bitcast.580, bf16[]{:T(256)} %bitcast.579, bf16[]{:T(256)} %bitcast.578, bf16[]{:T(256)} %bitcast.577, bf16[]{:T(256)} %bitcast.576, bf16[]{:T(256)} %bitcast.575, bf16[]{:T(256)} %bitcast.574, bf16[]{:T(256)} %bitcast.573, bf16[]{:T(256)} %bitcast.572, ...), kind=kLoop, calls=%fused_computation.241 | loop fusion | flops 179200 | bytes 10274 | tf_op jit(solution)/shard_map/convert_element_type | solution.py:59
  101.4 7.2 pad_maximum_fusion
  127.0 10.3 %slice.2561 = f32[32,32,64]{2,1,0:T(8,128)S(1)} slice(f32[32,32,134]{2,1,0:T(8,128)S(1)} %subtract_multiply_fusion.1), slice={[0:32:1], [0:32:1], [6:134:2]} | slice | bytes 524288 | tf_op jit(solution)/shard_map/slice | solution.py:25
  137.3 10.6 %slice.2560 = f32[32,32,64]{2,1,0:T(8,128)} slice(f32[32,32,134]{2,1,0:T(8,128)S(1)} %subtract_multiply_fusion.1), slice={[0:32:1], [0:32:1], [0:128:2]} | slice | bytes 524288 | tf_op jit(solution)/shard_map/slice | solution.py:25
  147.8 10.7 %slice.2559 = f32[32,32,64]{2,1,0:T(8,128)} slice(f32[32,32,134]{2,1,0:T(8,128)S(1)} %subtract_multiply_fusion.1), slice={[0:32:1], [0:32:1], [4:132:2]} | slice | bytes 524288 | tf_op jit(solution)/shard_map/slice | solution.py:25
  158.5 10.7 %slice.2558 = f32[32,32,64]{2,1,0:T(8,128)} slice(f32[32,32,134]{2,1,0:T(8,128)S(1)} %subtract_multiply_fusion.1), slice={[0:32:1], [0:32:1], [2:130:2]} | slice | bytes 524288 | tf_op jit(solution)/shard_map/slice | solution.py:25
  169.2 10.9 %slice.2557 = f32[32,32,64]{2,1,0:T(8,128)} slice(f32[32,32,134]{2,1,0:T(8,128)S(1)} %subtract_multiply_fusion.1), slice={[0:32:1], [0:32:1], [3:131:2]} | slice | bytes 524288 | tf_op jit(solution)/shard_map/slice | solution.py:25
  240.6 5.4 collective-permute-done.35
  278.1 12.8 %fusion.14 = bf16[80,64,128]{2,1,0:T(8,128)(2,1)} fusion(bf16[80,80,128]{1,2,0:T(8,128)(2,1)S(1)} %bitcast.800, bf16[]{:T(256)} %bitcast.617, bf16[]{:T(256)} %bitcast.616, bf16[]{:T(256)} %bitcast.615, bf16[]{:T(256)} %bitcast.614, bf16[]{:T(256)} %bitcast.613, bf16[]{:T(256)} %bitcast.612, bf16[]{:T(256)} %bitcast.611, bf16[]{:T(256)} %bitcast.610, ...), kind=kOutput, calls=%fused_computation.33 | convolution fusion | flops 105692160 | bytes 2949154 | tf_op jit(solution)/shard_map/abc,bw->awc/dot_general | solution.py:77
  292.6 12.8 %fusion.13 = bf16[80,64,128]{2,1,0:T(8,128)(2,1)} fusion(bf16[80,80,128]{1,2,0:T(8,128)(2,1)S(1)} %bitcast.801, bf16[]{:T(256)} %bitcast.599, bf16[]{:T(256)} %bitcast.598, bf16[]{:T(256)} %bitcast.597, bf16[]{:T(256)} %bitcast.596, bf16[]{:T(256)} %bitcast.595, bf16[]{:T(256)} %bitcast.594, bf16[]{:T(256)} %bitcast.593, bf16[]{:T(256)} %bitcast.592, ...), kind=kOutput, calls=%fused_computation.32 | convolution fusion | flops 105692160 | bytes 2949154 | tf_op jit(solution)/shard_map/abc,bw->awc/dot_general | solution.py:77
  307.1 11.6 %fusion.12 = bf16[80,64,128]{2,1,0:T(8,128)(2,1)S(1)} fusion(bf16[80,80,128]{1,2,0:T(8,128)(2,1)S(1)} %bitcast.802, bf16[]{:T(256)} %bitcast.581, bf16[]{:T(256)} %bitcast.580, bf16[]{:T(256)} %bitcast.579, bf16[]{:T(256)} %bitcast.578, bf16[]{:T(256)} %bitcast.577, bf16[]{:T(256)} %bitcast.576, bf16[]{:T(256)} %bitcast.575, bf16[]{:T(256)} %bitcast.574, ...), kind=kOutput, calls=%fused_computation.31 | convolution fusion | flops 105692160 | bytes 2949154 | tf_op jit(solution)/shard_map/abc,bw->awc/dot_general | solution.py:77
  320.4 12.9 %fusion.15 = bf16[80,64,128]{2,1,0:T(8,128)(2,1)} fusion(bf16[80,80,128]{1,2,0:T(8,128)(2,1)S(1)} %bitcast.799, bf16[]{:T(256)} %bitcast.635, bf16[]{:T(256)} %bitcast.634, bf16[]{:T(256)} %bitcast.633, bf16[]{:T(256)} %bitcast.632, bf16[]{:T(256)} %bitcast.631, bf16[]{:T(256)} %bitcast.630, bf16[]{:T(256)} %bitcast.629, bf16[]{:T(256)} %bitcast.628, ...), kind=kOutput, calls=%fused_computation.34 | convolution fusion | flops 105692160 | bytes 2949154 | tf_op jit(solution)/shard_map/abc,bw->awc/dot_general | solution.py:77
  334.7 11.1 %fusion.44 = bf16[32,16,32]{2,1,0:T(8,128)(2,1)S(1)} fusion(bf16[32,32,48]{2,1,0:T(8,128)(2,1)S(1)} %pad_maximum_fusion.21, bf16[]{:T(256)} %bitcast.275, bf16[]{:T(256)} %bitcast.274, bf16[]{:T(256)} %bitcast.273, bf16[]{:T(256)} %bitcast.272, bf16[]{:T(256)} %bitcast.271, bf16[]{:T(256)} %bitcast.270, bf16[]{:T(256)} %bitcast.269, bf16[]{:T(256)} %bitcast.268, ...), kind=kOutput, calls=%fused_computation.79 | convolution fusion | flops 4315136 | bytes 131106 | tf_op jit(solution)/shard_map/abc,bw->awc/dot_general | solution.py:77
  345.8 10.8 %fusion.99 = f32[16,16,32]{2,0,1:T(8,128)S(1)} fusion(bf16[32,16,32]{2,1,0:T(8,128)(2,1)S(1)} %fusion.44, bf16[]{:T(256)} %bitcast.275, bf16[]{:T(256)} %bitcast.274, bf16[]{:T(256)} %bitcast.273, bf16[]{:T(256)} %bitcast.272, bf16[]{:T(256)} %bitcast.271, bf16[]{:T(256)} %bitcast.270, bf16[]{:T(256)} %bitcast.269, bf16[]{:T(256)} %bitcast.268, ...), kind=kOutput, calls=%fused_computation.194 | convolution fusion | flops 542208 | bytes 65570 | tf_op jit(solution)/shard_map/abc,aw->wbc/dot_general | solution.py:77
  356.6 11.0 %fusion.45 = bf16[32,16,32]{2,1,0:T(8,128)(2,1)S(1)} fusion(bf16[32,32,48]{2,1,0:T(8,128)(2,1)S(1)} %pad_maximum_fusion.21, bf16[]{:T(256)} %bitcast.312, bf16[]{:T(256)} %bitcast.311, bf16[]{:T(256)} %bitcast.310, bf16[]{:T(256)} %bitcast.309, bf16[]{:T(256)} %bitcast.308, bf16[]{:T(256)} %bitcast.307, bf16[]{:T(256)} %bitcast.306, bf16[]{:T(256)} %bitcast.305, ...), kind=kOutput, calls=%fused_computation.80 | convolution fusion | flops 4315136 | bytes 131106 | tf_op jit(solution)/shard_map/abc,bw->awc/dot_general | solution.py:77
  367.6 10.8 %convolution_add_fusion.5 = f32[16,16,32]{2,0,1:T(8,128)S(1)} fusion(f32[16,16,32]{2,0,1:T(8,128)S(1)} %fusion.99, bf16[32,16,32]{2,1,0:T(8,128)(2,1)S(1)} %fusion.45, bf16[]{:T(256)} %bitcast.312, bf16[]{:T(256)} %bitcast.311, bf16[]{:T(256)} %bitcast.310, bf16[]{:T(256)} %bitcast.309, bf16[]{:T(256)} %bitcast.308, bf16[]{:T(256)} %bitcast.307, ...), kind=kOutput, calls=%fused_computation.85 | convolution fusion | flops 550400 | bytes 98338 | tf_op jit(solution)/shard_map/abc,aw->wbc/dot_general | solution.py:77
  378.4 10.9 %fusion.46 = bf16[32,16,32]{2,1,0:T(8,128)(2,1)S(1)} fusion(bf16[32,32,48]{2,1,0:T(8,128)(2,1)S(1)} %pad_maximum_fusion.21, bf16[]{:T(256)} %bitcast.349, bf16[]{:T(256)} %bitcast.348, bf16[]{:T(256)} %bitcast.347, bf16[]{:T(256)} %bitcast.346, bf16[]{:T(256)} %bitcast.345, bf16[]{:T(256)} %bitcast.344, bf16[]{:T(256)} %bitcast.343, bf16[]{:T(256)} %bitcast.342, ...), kind=kOutput, calls=%fused_computation.81 | convolution fusion | flops 4315136 | bytes 131106 | tf_op jit(solution)/shard_map/abc,bw->awc/dot_general | solution.py:77
  389.3 11.3 %convolution_add_fusion.4 = f32[16,16,32]{2,0,1:T(8,128)} fusion(f32[16,16,32]{2,0,1:T(8,128)S(1)} %convolution_add_fusion.5, bf16[32,16,32]{2,1,0:T(8,128)(2,1)S(1)} %fusion.46, bf16[]{:T(256)} %bitcast.349, bf16[]{:T(256)} %bitcast.348, bf16[]{:T(256)} %bitcast.347, bf16[]{:T(256)} %bitcast.346, bf16[]{:T(256)} %bitcast.345, bf16[]{:T(256)} %bitcast.344, ...), kind=kOutput, calls=%fused_computation.84 | convolution fusion | flops 550400 | bytes 98338 | tf_op jit(solution)/shard_map/abc,aw->wbc/dot_general | solution.py:77
  400.6 11.9 %fusion.47 = bf16[32,16,32]{2,1,0:T(8,128)(2,1)} fusion(bf16[32,32,48]{2,1,0:T(8,128)(2,1)S(1)} %pad_maximum_fusion.21, bf16[]{:T(256)} %bitcast.386, bf16[]{:T(256)} %bitcast.385, bf16[]{:T(256)} %bitcast.384, bf16[]{:T(256)} %bitcast.383, bf16[]{:T(256)} %bitcast.382, bf16[]{:T(256)} %bitcast.381, bf16[]{:T(256)} %bitcast.380, bf16[]{:T(256)} %bitcast.379, ...), kind=kOutput, calls=%fused_computation.82 | convolution fusion | flops 4315136 | bytes 131106 | tf_op jit(solution)/shard_map/abc,bw->awc/dot_general | solution.py:77
  417.3 11.1 %fusion.35 = bf16[48,32,64]{2,1,0:T(8,128)(2,1)S(1)} fusion(bf16[48,48,80]{2,1,0:T(8,128)(2,1)S(1)} %pad_maximum_fusion.14, bf16[]{:T(256)} %bitcast.127, bf16[]{:T(256)} %bitcast.126, bf16[]{:T(256)} %bitcast.125, bf16[]{:T(256)} %bitcast.124, bf16[]{:T(256)} %bitcast.123, bf16[]{:T(256)} %bitcast.122, bf16[]{:T(256)} %bitcast.121, bf16[]{:T(256)} %bitcast.120, ...), kind=kOutput, calls=%fused_computation.61 | convolution fusion | flops 33508864 | bytes 565282 | tf_op jit(solution)/shard_map/abc,bw->awc/dot_general | solution.py:77
  428.4 10.7 %fusion.72 = f32[32,32,64]{2,0,1:T(8,128)S(1)} fusion(bf16[48,32,64]{2,1,0:T(8,128)(2,1)S(1)} %fusion.35, bf16[]{:T(256)} %bitcast.127, bf16[]{:T(256)} %bitcast.126, bf16[]{:T(256)} %bitcast.125, bf16[]{:T(256)} %bitcast.124, bf16[]{:T(256)} %bitcast.123, bf16[]{:T(256)} %bitcast.122, bf16[]{:T(256)} %bitcast.121, bf16[]{:T(256)} %bitcast.120, ...), kind=kOutput, calls=%fused_computation.145 | convolution fusion | flops 6345216 | bytes 458786 | tf_op jit(solution)/shard_map/abc,aw->wbc/dot_general | solution.py:77
  439.1 11.8 %fusion.34 = bf16[48,32,64]{2,1,0:T(8,128)(2,1)} fusion(bf16[48,48,80]{2,1,0:T(8,128)(2,1)S(1)} %pad_maximum_fusion.14, bf16[]{:T(256)} %bitcast.164, bf16[]{:T(256)} %bitcast.163, bf16[]{:T(256)} %bitcast.162, bf16[]{:T(256)} %bitcast.161, bf16[]{:T(256)} %bitcast.160, bf16[]{:T(256)} %bitcast.159, bf16[]{:T(256)} %bitcast.158, bf16[]{:T(256)} %bitcast.157, ...), kind=kOutput, calls=%fused_computation.60 | convolution fusion | flops 33508864 | bytes 565282 | tf_op jit(solution)/shard_map/abc,bw->awc/dot_general | solution.py:77
  450.9 11.7 %convolution_add_fusion.2 = f32[32,32,64]{2,0,1:T(8,128)S(1)} fusion(f32[32,32,64]{2,0,1:T(8,128)S(1)} %fusion.72, bf16[48,32,64]{2,1,0:T(8,128)(2,1)} %fusion.34, bf16[]{:T(256)} %bitcast.164, bf16[]{:T(256)} %bitcast.163, bf16[]{:T(256)} %bitcast.162, bf16[]{:T(256)} %bitcast.161, bf16[]{:T(256)} %bitcast.160, bf16[]{:T(256)} %bitcast.159, ...), kind=kOutput, calls=%fused_computation.57 | convolution fusion | flops 6410752 | bytes 720930 | tf_op jit(solution)/shard_map/abc,aw->wbc/dot_general | solution.py:77
  470.0 11.1 %convolution_convert_fusion.13 = bf16[28,28,20]{1,2,0:T(8,128)(2,1)S(1)} fusion(bf16[28,28,36]{2,1,0:T(8,128)(2,1)S(1)} %fusion.79, bf16[]{:T(256)} %bitcast.498, bf16[]{:T(256)} %bitcast.497, bf16[]{:T(256)} %bitcast.496, bf16[]{:T(256)} %bitcast.495, bf16[]{:T(256)} %bitcast.494, bf16[]{:T(256)} %bitcast.493, bf16[]{:T(256)} %bitcast.492, bf16[]{:T(256)} %bitcast.491, ...), kind=kOutput, calls=%fused_computation.72 | convolution fusion | flops 1169840 | bytes 87842 | tf_op jit(solution)/shard_map/abc,cw->abw/dot_general | solution.py:77
  481.1 11.0 %fusion.51 = bf16[28,12,20]{0,1,2:T(8,128)(2,1)S(1)} fusion(bf16[28,28,20]{1,2,0:T(8,128)(2,1)S(1)} %convolution_convert_fusion.13, bf16[]{:T(256)} %bitcast.498, bf16[]{:T(256)} %bitcast.497, bf16[]{:T(256)} %bitcast.496, bf16[]{:T(256)} %bitcast.495, bf16[]{:T(256)} %bitcast.494, bf16[]{:T(256)} %bitcast.493, bf16[]{:T(256)} %bitcast.492, bf16[]{:T(256)} %bitcast.491, ...), kind=kOutput, calls=%fused_computation.96 | convolution fusion | flops 394800 | bytes 44834 | tf_op jit(solution)/shard_map/abc,bw->awc/dot_general | solution.py:77
  492.1 11.0 %convolution_convert_fusion.14 = bf16[28,28,20]{1,2,0:T(8,128)(2,1)S(1)} fusion(bf16[28,28,36]{2,1,0:T(8,128)(2,1)S(1)} %fusion.79, bf16[]{:T(256)} %bitcast.461, bf16[]{:T(256)} %bitcast.460, bf16[]{:T(256)} %bitcast.459, bf16[]{:T(256)} %bitcast.458, bf16[]{:T(256)} %bitcast.457, bf16[]{:T(256)} %bitcast.456, bf16[]{:T(256)} %bitcast.455, bf16[]{:T(256)} %bitcast.454, ...), kind=kOutput, calls=%fused_computation.73 | convolution fusion | flops 1169840 | bytes 87842 | tf_op jit(solution)/shard_map/abc,cw->abw/dot_general | solution.py:77
  503.2 10.9 %fusion.50 = bf16[28,12,20]{0,1,2:T(8,128)(2,1)S(1)} fusion(bf16[28,28,20]{1,2,0:T(8,128)(2,1)S(1)} %convolution_convert_fusion.14, bf16[]{:T(256)} %bitcast.461, bf16[]{:T(256)} %bitcast.460, bf16[]{:T(256)} %bitcast.459, bf16[]{:T(256)} %bitcast.458, bf16[]{:T(256)} %bitcast.457, bf16[]{:T(256)} %bitcast.456, bf16[]{:T(256)} %bitcast.455, bf16[]{:T(256)} %bitcast.454, ...), kind=kOutput, calls=%fused_computation.95 | convolution fusion | flops 394800 | bytes 44834 | tf_op jit(solution)/shard_map/abc,bw->awc/dot_general | solution.py:77
  514.1 11.0 %convolution_convert_fusion.15 = bf16[28,28,20]{1,2,0:T(8,128)(2,1)S(1)} fusion(bf16[28,28,36]{2,1,0:T(8,128)(2,1)S(1)} %fusion.79, bf16[]{:T(256)} %bitcast.424, bf16[]{:T(256)} %bitcast.423, bf16[]{:T(256)} %bitcast.422, bf16[]{:T(256)} %bitcast.421, bf16[]{:T(256)} %bitcast.420, bf16[]{:T(256)} %bitcast.419, bf16[]{:T(256)} %bitcast.418, bf16[]{:T(256)} %bitcast.417, ...), kind=kOutput, calls=%fused_computation.74 | convolution fusion | flops 1169840 | bytes 87842 | tf_op jit(solution)/shard_map/abc,cw->abw/dot_general | solution.py:77
  525.1 10.9 %fusion.49 = bf16[28,12,20]{0,1,2:T(8,128)(2,1)S(1)} fusion(bf16[28,28,20]{1,2,0:T(8,128)(2,1)S(1)} %convolution_convert_fusion.15, bf16[]{:T(256)} %bitcast.424, bf16[]{:T(256)} %bitcast.423, bf16[]{:T(256)} %bitcast.422, bf16[]{:T(256)} %bitcast.421, bf16[]{:T(256)} %bitcast.420, bf16[]{:T(256)} %bitcast.419, bf16[]{:T(256)} %bitcast.418, bf16[]{:T(256)} %bitcast.417, ...), kind=kOutput, calls=%fused_computation.94 | convolution fusion | flops 394800 | bytes 44834 | tf_op jit(solution)/shard_map/abc,bw->awc/dot_general | solution.py:77
  535.9 11.1 %convolution_convert_fusion.12 = bf16[28,28,20]{1,2,0:T(8,128)(2,1)S(1)} fusion(bf16[28,28,36]{2,1,0:T(8,128)(2,1)S(1)} %fusion.79, bf16[]{:T(256)} %bitcast.535, bf16[]{:T(256)} %bitcast.534, bf16[]{:T(256)} %bitcast.533, bf16[]{:T(256)} %bitcast.532, bf16[]{:T(256)} %bitcast.531, bf16[]{:T(256)} %bitcast.530, bf16[]{:T(256)} %bitcast.529, bf16[]{:T(256)} %bitcast.528, ...), kind=kOutput, calls=%fused_computation.71 | convolution fusion | flops 1169840 | bytes 87842 | tf_op jit(solution)/shard_map/abc,cw->abw/dot_general | solution.py:77
  547.0 11.0 %fusion.52 = bf16[28,12,20]{0,1,2:T(8,128)(2,1)S(1)} fusion(bf16[28,28,20]{1,2,0:T(8,128)(2,1)S(1)} %convolution_convert_fusion.12, bf16[]{:T(256)} %bitcast.535, bf16[]{:T(256)} %bitcast.534, bf16[]{:T(256)} %bitcast.533, bf16[]{:T(256)} %bitcast.532, bf16[]{:T(256)} %bitcast.531, bf16[]{:T(256)} %bitcast.530, bf16[]{:T(256)} %bitcast.529, bf16[]{:T(256)} %bitcast.528, ...), kind=kOutput, calls=%fused_computation.97 | convolution fusion | flops 394800 | bytes 44834 | tf_op jit(solution)/shard_map/abc,bw->awc/dot_general | solution.py:77
  558.0 10.8 %fusion.104 = f32[12,12,20]{2,0,1:T(8,128)S(1)} fusion(bf16[28,12,20]{0,1,2:T(8,128)(2,1)S(1)} %fusion.49, bf16[]{:T(256)} %bitcast.424, bf16[]{:T(256)} %bitcast.423, bf16[]{:T(256)} %bitcast.422, bf16[]{:T(256)} %bitcast.421, bf16[]{:T(256)} %bitcast.420, bf16[]{:T(256)} %bitcast.419, bf16[]{:T(256)} %bitcast.418, bf16[]{:T(256)} %bitcast.417, ...), kind=kOutput, calls=%fused_computation.210 | convolution fusion | flops 173040 | bytes 24994 | tf_op jit(solution)/shard_map/abc,aw->wbc/dot_general | solution.py:77
  568.8 10.9 %convolution_add_fusion.8 = f32[12,12,20]{2,0,1:T(8,128)S(1)} fusion(f32[12,12,20]{2,0,1:T(8,128)S(1)} %fusion.104, bf16[28,12,20]{0,1,2:T(8,128)(2,1)S(1)} %fusion.50, bf16[]{:T(256)} %bitcast.461, bf16[]{:T(256)} %bitcast.460, bf16[]{:T(256)} %bitcast.459, bf16[]{:T(256)} %bitcast.458, bf16[]{:T(256)} %bitcast.457, bf16[]{:T(256)} %bitcast.456, ...), kind=kOutput, calls=%fused_computation.93 | convolution fusion | flops 175920 | bytes 36514 | tf_op jit(solution)/shard_map/abc,aw->wbc/dot_general | solution.py:77
  579.7 10.9 %convolution_add_fusion.7 = f32[12,12,20]{2,0,1:T(8,128)S(1)} fusion(f32[12,12,20]{2,0,1:T(8,128)S(1)} %convolution_add_fusion.8, bf16[28,12,20]{0,1,2:T(8,128)(2,1)S(1)} %fusion.51, bf16[]{:T(256)} %bitcast.498, bf16[]{:T(256)} %bitcast.497, bf16[]{:T(256)} %bitcast.496, bf16[]{:T(256)} %bitcast.495, bf16[]{:T(256)} %bitcast.494, bf16[]{:T(256)} %bitcast.493, ...), kind=kOutput, calls=%fused_computation.92 | convolution fusion | flops 175920 | bytes 36514 | tf_op jit(solution)/shard_map/abc,aw->wbc/dot_general | solution.py:77
  590.6 10.9 %convolution_add_fusion.6 = f32[12,12,20]{2,0,1:T(8,128)S(1)} fusion(f32[12,12,20]{2,0,1:T(8,128)S(1)} %convolution_add_fusion.7, bf16[28,12,20]{0,1,2:T(8,128)(2,1)S(1)} %fusion.52, bf16[]{:T(256)} %bitcast.535, bf16[]{:T(256)} %bitcast.534, bf16[]{:T(256)} %bitcast.533, bf16[]{:T(256)} %bitcast.532, bf16[]{:T(256)} %bitcast.531, bf16[]{:T(256)} %bitcast.530, ...), kind=kOutput, calls=%fused_computation.91 | convolution fusion | flops 175920 | bytes 36514 | tf_op jit(solution)/shard_map/abc,aw->wbc/dot_general | solution.py:77
  602.4 10.8 %fusion.48 = f32[16,16,32]{2,0,1:T(8,128)S(1)} fusion(f32[16,16,32]{2,0,1:T(8,128)S(1)} %copy.198, f32[16,16,32]{2,0,1:T(8,128)S(1)} %copy-done.16, bf16[32,16,32]{2,1,0:T(8,128)(2,1)S(1)} %copy-done.32, bf16[]{:T(256)} %bitcast.386, bf16[]{:T(256)} %bitcast.385, bf16[]{:T(256)} %bitcast.384, bf16[]{:T(256)} %bitcast.383, bf16[]{:T(256)} %bitcast.382, ...), kind=kOutput, calls=%fused_computation.86 | convolution fusion | flops 558592 | bytes 131106 | tf_op jit(solution)/shard_map/abc,aw->wbc/dot_general | solution.py:77
  617.1 11.1 %fusion.33 = bf16[48,32,64]{2,1,0:T(8,128)(2,1)S(1)} fusion(bf16[48,48,80]{2,1,0:T(8,128)(2,1)S(1)} %pad_maximum_fusion.14, bf16[]{:T(256)} %bitcast.201, bf16[]{:T(256)} %bitcast.200, bf16[]{:T(256)} %bitcast.199, bf16[]{:T(256)} %bitcast.198, bf16[]{:T(256)} %bitcast.197, bf16[]{:T(256)} %bitcast.196, bf16[]{:T(256)} %bitcast.195, bf16[]{:T(256)} %bitcast.194, ...), kind=kOutput, calls=%fused_computation.59 | convolution fusion | flops 33508864 | bytes 565282 | tf_op jit(solution)/shard_map/abc,bw->awc/dot_general | solution.py:77
  630.3 11.6 %convolution_add_fusion.1 = f32[32,32,64]{2,0,1:T(8,128)} fusion(f32[32,32,64]{2,0,1:T(8,128)S(1)} %convolution_add_fusion.2, bf16[48,32,64]{2,1,0:T(8,128)(2,1)S(1)} %fusion.33, bf16[]{:T(256)} %bitcast.201, bf16[]{:T(256)} %bitcast.200, bf16[]{:T(256)} %bitcast.199, bf16[]{:T(256)} %bitcast.198, bf16[]{:T(256)} %bitcast.197, bf16[]{:T(256)} %bitcast.196, ...), kind=kOutput, calls=%fused_computation.56 | convolution fusion | flops 6410752 | bytes 720930 | tf_op jit(solution)/shard_map/abc,aw->wbc/dot_general | solution.py:77
  644.2 11.7 %fusion.32 = bf16[48,32,64]{2,1,0:T(8,128)(2,1)} fusion(bf16[48,48,80]{2,1,0:T(8,128)(2,1)S(1)} %pad_maximum_fusion.14, bf16[]{:T(256)} %bitcast.238, bf16[]{:T(256)} %bitcast.237, bf16[]{:T(256)} %bitcast.236, bf16[]{:T(256)} %bitcast.235, bf16[]{:T(256)} %bitcast.234, bf16[]{:T(256)} %bitcast.233, bf16[]{:T(256)} %bitcast.232, bf16[]{:T(256)} %bitcast.231, ...), kind=kOutput, calls=%fused_computation.58 | convolution fusion | flops 33508864 | bytes 565282 | tf_op jit(solution)/shard_map/abc,bw->awc/dot_general | solution.py:77
  662.2 11.9 %fusion.31 = f32[32,32,64]{2,0,1:T(8,128)S(1)} fusion(f32[32,32,64]{2,0,1:T(8,128)} %copy.204, f32[32,32,64]{2,0,1:T(8,128)} %convolution_add_fusion.1, bf16[48,32,64]{2,1,0:T(8,128)(2,1)} %fusion.32, bf16[]{:T(256)} %bitcast.238, bf16[]{:T(256)} %bitcast.237, bf16[]{:T(256)} %bitcast.236, bf16[]{:T(256)} %bitcast.235, bf16[]{:T(256)} %bitcast.234, ...), kind=kOutput, calls=%fused_computation.55 | convolution fusion | flops 6476288 | bytes 983074 | tf_op jit(solution)/shard_map/abc,aw->wbc/dot_general | solution.py:77
  678.0 13.1 %fusion.17 = f32[64,64,128]{2,0,1:T(8,128)} fusion(bf16[80,64,128]{2,1,0:T(8,128)(2,1)S(1)} %copy-done.5, bf16[]{:T(256)} %bitcast.617, bf16[]{:T(256)} %bitcast.616, bf16[]{:T(256)} %bitcast.615, bf16[]{:T(256)} %bitcast.614, bf16[]{:T(256)} %bitcast.613, bf16[]{:T(256)} %bitcast.612, bf16[]{:T(256)} %bitcast.611, bf16[]{:T(256)} %bitcast.610, ...), kind=kOutput, calls=%fused_computation.40 | convolution fusion | flops 84065280 | bytes 3407906 | tf_op jit(solution)/shard_map/abc,aw->wbc/dot_general | solution.py:77
  693.2 13.0 %fusion.19 = f32[64,64,128]{2,0,1:T(8,128)} fusion(bf16[80,64,128]{2,1,0:T(8,128)(2,1)S(1)} %copy-done.4, bf16[]{:T(256)} %bitcast.599, bf16[]{:T(256)} %bitcast.598, bf16[]{:T(256)} %bitcast.597, bf16[]{:T(256)} %bitcast.596, bf16[]{:T(256)} %bitcast.595, bf16[]{:T(256)} %bitcast.594, bf16[]{:T(256)} %bitcast.593, bf16[]{:T(256)} %bitcast.592, ...), kind=kOutput, calls=%fused_computation.42 | convolution fusion | flops 84065280 | bytes 3407906 | tf_op jit(solution)/shard_map/abc,aw->wbc/dot_general | solution.py:77
  711.4 13.0 %fusion.21 = f32[64,64,128]{2,0,1:T(8,128)} fusion(bf16[80,64,128]{2,1,0:T(8,128)(2,1)S(1)} %fusion.12, bf16[]{:T(256)} %bitcast.581, bf16[]{:T(256)} %bitcast.580, bf16[]{:T(256)} %bitcast.579, bf16[]{:T(256)} %bitcast.578, bf16[]{:T(256)} %bitcast.577, bf16[]{:T(256)} %bitcast.576, bf16[]{:T(256)} %bitcast.575, bf16[]{:T(256)} %bitcast.574, ...), kind=kOutput, calls=%fused_computation.44 | convolution fusion | flops 84065280 | bytes 3407906 | tf_op jit(solution)/shard_map/abc,aw->wbc/dot_general | solution.py:77
  732.6 6.2 copy.213
  743.4 15.0 %add_convert_fusion.4 = bf16[64,64,128]{2,0,1:T(8,128)(2,1)S(1)} fusion(f32[64,64,128]{2,0,1:T(8,128)S(1)} %copy.214, f32[64,64,128]{2,0,1:T(8,128)} %fusion.17, f32[64,64,128]{2,0,1:T(8,128)} %fusion.21, f32[64,64,128]{2,0,1:T(8,128)} %fusion.19, bf16[80,64,128]{2,1,0:T(8,128)(2,1)S(1)} %copy-done.3, bf16[]{:T(256)} %bitcast.635, bf16[]{:T(256)} %bitcast.634, ...), kind=kOutput, calls=%fused_computation.16 | convolution fusion | flops 86686720 | bytes 10747938 | tf_op jit(solution)/shard_map/abc,aw->wbc/dot_general | solution.py:77
  (332 shorter events, 226.2 us)
Async XLA Ops:
  1.5 66.9 %collective-permute-start.6 = (f32[3,64,128]{2,1,0:T(8,128)}, f32[3,64,128]{2,1,0:T(8,128)S(1)}, u32[]{:S(2)}, u32[]{:S(2)}) collective-permute-start(f32[3,64,128]{2,1,0:T(8,128)} %get-tuple-element.25), channel_id=1, source_target_pairs={{0,8},{8,16},{16,24},{24,0},{1,9},{9,17},{17,25},{25,1},{2,10},{10... | collective-permute-start | bytes 294920 | tf_op jit(solution)/shard_map/ppermute | solution.py:14
  4.6 63.9 %collective-permute-start.7 = (f32[3,64,128]{2,1,0:T(8,128)}, f32[3,64,128]{2,1,0:T(8,128)}, u32[]{:S(2)}, u32[]{:S(2)}) collective-permute-start(f32[3,64,128]{2,1,0:T(8,128)} %get-tuple-element.26), channel_id=1, source_target_pairs={{8,0},{16,8},{24,16},{0,24},{9,1},{17,9},{25,17},{1,25},{10,2},{18... | collective-permute-start | bytes 294920 | tf_op jit(solution)/shard_map/ppermute | solution.py:15
  8.2 62.8 %collective-permute-start.1 = (bf16[8,64,128]{2,1,0:T(8,128)(2,1)}, bf16[8,64,128]{2,1,0:T(8,128)(2,1)}, u32[]{:S(2)}, u32[]{:S(2)}) collective-permute-start(bf16[8,64,128]{2,1,0:T(8,128)(2,1)} %get-tuple-element.21), channel_id=1, source_target_pairs={{8,0},{16,8},{24,16},{0,24},{9,1},{17,9},{25,17},{1,25},{10,2},{18... | collective-permute-start | bytes 393224 | tf_op jit(solution)/shard_map/ppermute | solution.py:15
  10.3 56.2 %collective-permute-start = (bf16[8,64,128]{2,1,0:T(8,128)(2,1)S(1)}, bf16[8,64,128]{2,1,0:T(8,128)(2,1)S(1)}, u32[]{:S(2)}, u32[]{:S(2)}) collective-permute-start(bf16[8,64,128]{2,1,0:T(8,128)(2,1)S(1)} %get-tuple-element.22), channel_id=1, source_target_pairs={{0,8},{8,16},{16,24},{24,0},{1,9},{9,17},{17,25},{25,1},{2,10},{10... | collective-permute-start | bytes 393224 | tf_op jit(solution)/shard_map/ppermute | solution.py:14
  69.3 5.3 collective-permute-start.8
  69.3 5.3 collective-permute-start.9
  72.8 16.0 %collective-permute-start.2 = (bf16[80,8,128]{2,1,0:T(8,128)(2,1)}, bf16[80,8,128]{2,1,0:T(8,128)(2,1)}, u32[]{:S(2)}, u32[]{:S(2)}) collective-permute-start(bf16[80,8,128]{2,1,0:T(8,128)(2,1)} %get-tuple-element.17), channel_id=1, source_target_pairs={{0,2},{2,4},{4,6},{6,0},{1,3},{3,5},{5,7},{7,1},{8,10},{10,12},{12... | collective-permute-start | bytes 491528 | tf_op jit(solution)/shard_map/ppermute | solution.py:14
  72.9 15.9 %collective-permute-start.3 = (bf16[80,8,128]{2,1,0:T(8,128)(2,1)}, bf16[80,8,128]{2,1,0:T(8,128)(2,1)}, u32[]{:S(2)}, u32[]{:S(2)}) collective-permute-start(bf16[80,8,128]{2,1,0:T(8,128)(2,1)} %get-tuple-element.18), channel_id=1, source_target_pairs={{2,0},{4,2},{6,4},{0,6},{3,1},{5,3},{7,5},{1,7},{10,8},{12,10},{14... | collective-permute-start | bytes 491528 | tf_op jit(solution)/shard_map/ppermute | solution.py:15
  86.8 11.4 %collective-permute-start.11 = (f32[70,70,3]{1,0,2:T(8,128)}, f32[70,70,3]{1,0,2:T(8,128)}, u32[]{:S(2)}, u32[]{:S(2)}) collective-permute-start(f32[70,70,3]{1,0,2:T(8,128)} %copy.165), channel_id=1, source_target_pairs={{1,0},{0,1},{3,2},{2,3},{5,4},{4,5},{7,6},{6,7},{9,8},{8,9},{11,10... | collective-permute-start | bytes 176408 | tf_op jit(solution)/shard_map/ppermute | solution.py:15
  88.5 6.3 collective-permute-start.10
  181.9 12.0 %collective-permute-start.18 = (f32[3,32,64]{2,1,0:T(8,128)S(1)}, f32[3,32,64]{2,1,0:T(8,128)S(1)}, u32[]{:S(2)}, u32[]{:S(2)}) collective-permute-start(f32[3,32,64]{2,1,0:T(8,128)S(1)} %get-tuple-element.45), channel_id=1, source_target_pairs={{0,8},{8,16},{16,24},{24,0},{1,9},{9,17},{17,25},{25,1},{2,10},{10... | collective-permute-start | bytes 73736 | tf_op jit(solution)/shard_map/ppermute | solution.py:14
  182.0 11.9 %collective-permute-start.19 = (f32[3,32,64]{2,1,0:T(8,128)S(1)}, f32[3,32,64]{2,1,0:T(8,128)S(1)}, u32[]{:S(2)}, u32[]{:S(2)}) collective-permute-start(f32[3,32,64]{2,1,0:T(8,128)S(1)} %get-tuple-element.46), channel_id=1, source_target_pairs={{8,0},{16,8},{24,16},{0,24},{9,1},{17,9},{25,17},{1,25},{10,2},{18... | collective-permute-start | bytes 73736 | tf_op jit(solution)/shard_map/ppermute | solution.py:15
  191.9 71.2 %collective-permute-start.5 = (bf16[80,80,8]{1,2,0:T(8,128)(2,1)}, bf16[80,80,8]{1,2,0:T(8,128)(2,1)}, u32[]{:S(2)}, u32[]{:S(2)}) collective-permute-start(bf16[80,80,8]{1,2,0:T(8,128)(2,1)} %copy.148), channel_id=1, source_target_pairs={{1,0},{0,1},{3,2},{2,3},{5,4},{4,5},{7,6},{6,7},{9,8},{8,9},{11,10... | collective-permute-start | bytes 307208 | tf_op jit(solution)/shard_map/ppermute | solution.py:15
  193.4 65.6 %collective-permute-start.4 = (bf16[80,80,8]{1,2,0:T(8,128)(2,1)}, bf16[80,80,8]{1,2,0:T(8,128)(2,1)}, u32[]{:S(2)}, u32[]{:S(2)}) collective-permute-start(bf16[80,80,8]{1,2,0:T(8,128)(2,1)} %copy.147), channel_id=1, source_target_pairs={{0,1},{1,0},{2,3},{3,2},{4,5},{5,4},{6,7},{7,6},{8,9},{9,8},{10,11... | collective-permute-start | bytes 307208 | tf_op jit(solution)/shard_map/ppermute | solution.py:14
  194.0 3.9 collective-permute-start.20
  194.0 5.6 collective-permute-start.21
  195.8 6.6 collective-permute-start.12
  197.9 5.7 collective-permute-start.13
  200.8 6.2 collective-permute-start.23
  202.4 4.2 collective-permute-start.22
  203.6 23.6 %collective-permute-start.14 = (bf16[48,8,64]{2,1,0:T(8,128)(2,1)S(1)}, bf16[48,8,64]{2,1,0:T(8,128)(2,1)S(1)}, u32[]{:S(2)}, u32[]{:S(2)}) collective-permute-start(bf16[48,8,64]{2,1,0:T(8,128)(2,1)S(1)} %get-tuple-element.49), channel_id=1, source_target_pairs={{0,2},{2,4},{4,6},{6,0},{1,3},{3,5},{5,7},{7,1},{8,10},{10,12},{12... | collective-permute-start | bytes 147464 | tf_op jit(solution)/shard_map/ppermute | solution.py:14
  215.2 5.8 collective-permute-start.30
  215.4 5.5 collective-permute-start.31
  220.9 5.7 collective-permute-start.24
  220.9 5.7 collective-permute-start.25
  226.7 4.2 collective-permute-start.32
  227.2 3.7 collective-permute-start.33
  229.2 26.7 %collective-permute-start.26 = (bf16[32,8,32]{2,1,0:T(8,128)(2,1)S(1)}, bf16[32,8,32]{2,1,0:T(8,128)(2,1)S(1)}, u32[]{:S(2)}, u32[]{:S(2)}) collective-permute-start(bf16[32,8,32]{2,1,0:T(8,128)(2,1)S(1)} %get-tuple-element.71), channel_id=1, source_target_pairs={{0,2},{2,4},{4,6},{6,0},{1,3},{3,5},{5,7},{7,1},{8,10},{10,12},{12... | collective-permute-start | bytes 49160 | tf_op jit(solution)/shard_map/ppermute | solution.py:14
  231.1 9.4 %collective-permute-start.34 = (f32[22,22,3]{2,1,0:T(8,128)S(1)}, f32[22,22,3]{2,1,0:T(8,128)S(1)}, u32[]{:S(2)}, u32[]{:S(2)}) collective-permute-start(f32[22,22,3]{2,1,0:T(8,128)S(1)} %get-tuple-element.53), channel_id=1, source_target_pairs={{0,1},{1,0},{2,3},{3,2},{4,5},{5,4},{6,7},{7,6},{8,9},{9,8},{10,11... | collective-permute-start | bytes 17432 | tf_op jit(solution)/shard_map/ppermute | solution.py:14
  232.3 13.7 %collective-permute-start.35 = (f32[22,22,3]{2,1,0:T(8,128)S(1)}, f32[22,22,3]{2,1,0:T(8,128)S(1)}, u32[]{:S(2)}, u32[]{:S(2)}) collective-permute-start(f32[22,22,3]{2,1,0:T(8,128)S(1)} %get-tuple-element.54), channel_id=1, source_target_pairs={{1,0},{0,1},{3,2},{2,3},{5,4},{4,5},{7,6},{6,7},{9,8},{8,9},{11,10... | collective-permute-start | bytes 17432 | tf_op jit(solution)/shard_map/ppermute | solution.py:15
  240.6 17.1 %collective-permute-start.27 = (bf16[32,8,32]{2,1,0:T(8,128)(2,1)S(1)}, bf16[32,8,32]{2,1,0:T(8,128)(2,1)S(1)}, u32[]{:S(2)}, u32[]{:S(2)}) collective-permute-start(bf16[32,8,32]{2,1,0:T(8,128)(2,1)S(1)} %get-tuple-element.72), channel_id=1, source_target_pairs={{2,0},{4,2},{6,4},{0,6},{3,1},{5,3},{7,5},{1,7},{10,8},{12,10},{14... | collective-permute-start | bytes 49160 | tf_op jit(solution)/shard_map/ppermute | solution.py:15
  246.0 167.7 %collective-permute-start.17 = (bf16[48,48,8]{1,2,0:T(8,128)(2,1)}, bf16[48,48,8]{1,2,0:T(8,128)(2,1)}, u32[]{:S(2)}, u32[]{:S(2)}) collective-permute-start(bf16[48,48,8]{1,2,0:T(8,128)(2,1)} %copy.169), channel_id=1, source_target_pairs={{1,0},{0,1},{3,2},{2,3},{5,4},{4,5},{7,6},{6,7},{9,8},{8,9},{11,10... | collective-permute-start | bytes 110600 | tf_op jit(solution)/shard_map/ppermute | solution.py:15
  250.9 211.7 %all-to-all-start = ((bf16[32,2,512]{2,1,0:T(2,128)(2,1)}), bf16[32,2,512]{2,1,0:T(2,128)(2,1)}, u32[]{:S(2)}, u32[]{:S(2)}) async-start(bf16[32,2,512]{2,1,0:T(2,128)(2,1)} %reshape.1488), calls=%async_computation | async-start | bytes 131072 | tf_op jit(solution)/shard_map/all_to_all | solution.py:138
  255.9 156.6 %collective-permute-start.16 = (bf16[48,48,8]{1,2,0:T(8,128)(2,1)}, bf16[48,48,8]{1,2,0:T(8,128)(2,1)}, u32[]{:S(2)}, u32[]{:S(2)}) collective-permute-start(bf16[48,48,8]{1,2,0:T(8,128)(2,1)} %copy.168), channel_id=1, source_target_pairs={{0,1},{1,0},{2,3},{3,2},{4,5},{5,4},{6,7},{7,6},{8,9},{9,8},{10,11... | collective-permute-start | bytes 110600 | tf_op jit(solution)/shard_map/ppermute | solution.py:14
  258.7 74.7 %collective-permute-start.28 = (bf16[32,32,8]{2,1,0:T(8,128)(2,1)}, bf16[32,32,8]{2,1,0:T(8,128)(2,1)}, u32[]{:S(2)}, u32[]{:S(2)}) collective-permute-start(bf16[32,32,8]{2,1,0:T(8,128)(2,1)} %get-tuple-element.57), channel_id=1, source_target_pairs={{0,1},{1,0},{2,3},{3,2},{4,5},{5,4},{6,7},{7,6},{8,9},{9,8},{10,11... | collective-permute-start | bytes 49160 | tf_op jit(solution)/shard_map/ppermute | solution.py:14
  259.0 74.4 %collective-permute-start.29 = (bf16[32,32,8]{2,1,0:T(8,128)(2,1)}, bf16[32,32,8]{2,1,0:T(8,128)(2,1)}, u32[]{:S(2)}, u32[]{:S(2)}) collective-permute-start(bf16[32,32,8]{2,1,0:T(8,128)(2,1)} %get-tuple-element.58), channel_id=1, source_target_pairs={{1,0},{0,1},{3,2},{2,3},{5,4},{4,5},{7,6},{6,7},{9,8},{8,9},{11,10... | collective-permute-start | bytes 49160 | tf_op jit(solution)/shard_map/ppermute | solution.py:15
  613.2 15.0 %collective-permute-start.36 = (f32[2,16,32]{2,0,1:T(2,128)S(1)}, f32[2,16,32]{2,0,1:T(2,128)S(1)}, u32[]{:S(2)}, u32[]{:S(2)}) collective-permute-start(f32[2,16,32]{2,0,1:T(2,128)S(1)} %get-tuple-element.69), channel_id=1, source_target_pairs={{0,8},{8,16},{16,24},{24,0},{1,9},{9,17},{17,25},{25,1},{2,10},{10... | collective-permute-start | bytes 12296 | tf_op jit(solution)/shard_map/ppermute | solution.py:14
  614.7 13.5 %collective-permute-start.37 = (f32[2,16,32]{2,0,1:T(2,128)S(1)}, f32[2,16,32]{2,0,1:T(2,128)S(1)}, u32[]{:S(2)}, u32[]{:S(2)}) collective-permute-start(f32[2,16,32]{2,0,1:T(2,128)S(1)} %get-tuple-element.70), channel_id=1, source_target_pairs={{8,0},{16,8},{24,16},{0,24},{9,1},{17,9},{25,17},{1,25},{10,2},{18... | collective-permute-start | bytes 12296 | tf_op jit(solution)/shard_map/ppermute | solution.py:15
  628.3 13.6 %collective-permute-start.38 = (f32[20,2,32]{2,0,1:T(8,128)S(1)}, f32[20,2,32]{2,0,1:T(8,128)S(1)}, u32[]{:S(2)}, u32[]{:S(2)}) collective-permute-start(f32[20,2,32]{2,0,1:T(8,128)S(1)} %get-tuple-element.67), channel_id=1, source_target_pairs={{0,2},{2,4},{4,6},{6,0},{1,3},{3,5},{5,7},{7,1},{8,10},{10,12},{12... | collective-permute-start | bytes 15368 | tf_op jit(solution)/shard_map/ppermute | solution.py:14
  628.6 13.4 %collective-permute-start.39 = (f32[20,2,32]{2,0,1:T(8,128)S(1)}, f32[20,2,32]{2,0,1:T(8,128)S(1)}, u32[]{:S(2)}, u32[]{:S(2)}) collective-permute-start(f32[20,2,32]{2,0,1:T(8,128)S(1)} %get-tuple-element.68), channel_id=1, source_target_pairs={{2,0},{4,2},{6,4},{0,6},{3,1},{5,3},{7,5},{1,7},{10,8},{12,10},{14... | collective-permute-start | bytes 15368 | tf_op jit(solution)/shard_map/ppermute | solution.py:15
  642.1 13.8 %collective-permute-start.40 = (f32[20,20,2]{2,0,1:T(8,128)S(1)}, f32[20,20,2]{2,0,1:T(8,128)S(1)}, u32[]{:S(2)}, u32[]{:S(2)}) collective-permute-start(f32[20,20,2]{2,0,1:T(8,128)S(1)} %get-tuple-element.63), channel_id=1, source_target_pairs={{0,1},{1,0},{2,3},{3,2},{4,5},{5,4},{6,7},{7,6},{8,9},{9,8},{10,11... | collective-permute-start | bytes 9608 | tf_op jit(solution)/shard_map/ppermute | solution.py:14
  642.5 13.4 %collective-permute-start.41 = (f32[20,20,2]{2,0,1:T(8,128)S(1)}, f32[20,20,2]{2,0,1:T(8,128)S(1)}, u32[]{:S(2)}, u32[]{:S(2)}) collective-permute-start(f32[20,20,2]{2,0,1:T(8,128)S(1)} %get-tuple-element.64), channel_id=1, source_target_pairs={{1,0},{0,1},{3,2},{2,3},{5,4},{4,5},{7,6},{6,7},{9,8},{8,9},{11,10... | collective-permute-start | bytes 9608 | tf_op jit(solution)/shard_map/ppermute | solution.py:15
  674.2 17.0 %collective-permute-start.42 = (f32[2,32,64]{2,0,1:T(2,128)S(1)}, f32[2,32,64]{2,0,1:T(2,128)S(1)}, u32[]{:S(2)}, u32[]{:S(2)}) collective-permute-start(f32[2,32,64]{2,0,1:T(2,128)S(1)} %get-tuple-element.41), channel_id=1, source_target_pairs={{0,8},{8,16},{16,24},{24,0},{1,9},{9,17},{17,25},{25,1},{2,10},{10... | collective-permute-start | bytes 49160 | tf_op jit(solution)/shard_map/ppermute | solution.py:14
  674.2 16.9 %collective-permute-start.43 = (f32[2,32,64]{2,0,1:T(2,128)S(1)}, f32[2,32,64]{2,0,1:T(2,128)S(1)}, u32[]{:S(2)}, u32[]{:S(2)}) collective-permute-start(f32[2,32,64]{2,0,1:T(2,128)S(1)} %get-tuple-element.42), channel_id=1, source_target_pairs={{8,0},{16,8},{24,16},{0,24},{9,1},{17,9},{25,17},{1,25},{10,2},{18... | collective-permute-start | bytes 49160 | tf_op jit(solution)/shard_map/ppermute | solution.py:15
  691.2 15.1 %collective-permute-start.44 = (f32[36,2,64]{2,0,1:T(8,128)S(1)}, f32[36,2,64]{2,0,1:T(8,128)S(1)}, u32[]{:S(2)}, u32[]{:S(2)}) collective-permute-start(f32[36,2,64]{2,0,1:T(8,128)S(1)} %get-tuple-element.37), channel_id=1, source_target_pairs={{0,2},{2,4},{4,6},{6,0},{1,3},{3,5},{5,7},{7,1},{8,10},{10,12},{12... | collective-permute-start | bytes 55304 | tf_op jit(solution)/shard_map/ppermute | solution.py:14
  691.3 15.0 %collective-permute-start.45 = (f32[36,2,64]{2,0,1:T(8,128)S(1)}, f32[36,2,64]{2,0,1:T(8,128)S(1)}, u32[]{:S(2)}, u32[]{:S(2)}) collective-permute-start(f32[36,2,64]{2,0,1:T(8,128)S(1)} %get-tuple-element.38), channel_id=1, source_target_pairs={{2,0},{4,2},{6,4},{0,6},{3,1},{5,3},{7,5},{1,7},{10,8},{12,10},{14... | collective-permute-start | bytes 55304 | tf_op jit(solution)/shard_map/ppermute | solution.py:15
  709.3 15.5 %collective-permute-start.47 = (f32[36,36,2]{1,2,0:T(2,128)S(1)}, f32[36,36,2]{1,2,0:T(2,128)S(1)}, u32[]{:S(2)}, u32[]{:S(2)}) collective-permute-start(f32[36,36,2]{1,2,0:T(2,128)S(1)} %copy.206), channel_id=1, source_target_pairs={{1,0},{0,1},{3,2},{2,3},{5,4},{4,5},{7,6},{6,7},{9,8},{8,9},{11,10... | collective-permute-start | bytes 31112 | tf_op jit(solution)/shard_map/ppermute | solution.py:15
  709.7 14.7 %collective-permute-start.46 = (f32[36,36,2]{1,2,0:T(2,128)S(1)}, f32[36,36,2]{1,2,0:T(2,128)S(1)}, u32[]{:S(2)}, u32[]{:S(2)}) collective-permute-start(f32[36,36,2]{1,2,0:T(2,128)S(1)} %copy.205), channel_id=1, source_target_pairs={{0,1},{1,0},{2,3},{3,2},{4,5},{5,4},{6,7},{7,6},{8,9},{9,8},{10,11... | collective-permute-start | bytes 31112 | tf_op jit(solution)/shard_map/ppermute | solution.py:14
  (34 other events, 768.0 us)
